TPU v7x, 32 devices: a whole 2x2x4 slice. The times are simulated.
32 devices in a mesh: dp: 16 (over z, y, core), mp: 2 (over x).
Axes of the slice: x: 2, y: 2, z: 4, core: 2. Of those that a mesh axis runs over, the one named last changes fastest.
Arguments:
- images: bfloat16 [64, 196, 512], P('dp'), may hold values from -6 to 6
- loads: int32 [16], P('dp'), may hold values from 1 to 4, as said below
- cotangent: bfloat16 [64, 196, 512], P('dp'), may hold values from -6 to 6
- ln1_gain: float32 [2, 512], replicated, may hold values from 0.5 to 1.5
- ln1_bias: float32 [2, 512], replicated, may hold values from -3 to 3
- w_qkv: bfloat16 [2, 512, 3, 512], P(None, 'dp', None, 'mp'), may hold values from -0.25 to 0.25
- qv_bias: float32 [2, 2, 512], P(None, None, 'mp'), may hold values from -3 to 3
- rel_table: float32 [2, 16, 169], P(None, 'mp'), may hold values from -4 to 330
- w_proj: bfloat16 [2, 512, 512], P(None, 'mp', 'dp'), may hold values from -0.75 to 0.75
- proj_bias: float32 [2, 512], replicated, may hold values from -3 to 3
- ln2_gain: float32 [2, 512], replicated, may hold values from 0.5 to 1.5
- ln2_bias: float32 [2, 512], replicated, may hold values from -3 to 3
- w_fc1: bfloat16 [2, 512, 2048], P(None, 'dp', 'mp'), may hold values from -0.25 to 0.25
- fc1_bias: float32 [2, 2048], P(None, 'mp'), may hold values from -3 to 3
- w_fc2: bfloat16 [2, 2048, 512], P(None, 'mp', 'dp'), may hold values from -0.1875 to 0.1875
- fc2_bias: float32 [2, 512], replicated, may hold values from -3 to 3
Outputs:
- result: bfloat16 [64, 196, 512], P('dp')
- images_grad: bfloat16 [64, 196, 512], P('dp')
- ln1_gain_grad: float32 [2, 512], replicated
- ln1_bias_grad: float32 [2, 512], replicated
- w_qkv_grad: float32 [2, 512, 3, 512], P(None, 'dp', None, 'mp')
- qv_bias_grad: float32 [2, 2, 512], P(None, None, 'mp')
- rel_table_grad: float32 [2, 16, 169], P(None, 'mp')
- w_proj_grad: float32 [2, 512, 512], P(None, 'mp', 'dp')
- proj_bias_grad: float32 [2, 512], replicated
- ln2_gain_grad: float32 [2, 512], replicated
- ln2_bias_grad: float32 [2, 512], replicated
- w_fc1_grad: float32 [2, 512, 2048], P(None, 'dp', 'mp')
- fc1_bias_grad: float32 [2, 2048], P(None, 'mp')
- w_fc2_grad: float32 [2, 2048, 512], P(None, 'mp', 'dp')
- fc2_bias_grad: float32 [2, 512], replicated
Inputs may be any that keep to these rules, and one draw needn't show every extreme that they name: `loads`: some index of dp uses all 4 slots.
All inputs are finite; a program needn't handle non-finite values.
Results may differ from a plain program's by a relative error of at most 0.02.
Values may be sent and summed in bfloat16 or wider, within the bound.
A program may use at most 192 MiB of HBM per device.

v0:
```python
import jax
import jax.numpy as jnp
from jax import lax
from jax.sharding import PartitionSpec as P

HD = 32
SIDE = 14
WIN = 7
SHIFT = 3
LAYERS = 2
MICRO = 2
TOK_IMG = 196


EPS = 1e-05
MASKED = -1e30
INV_ROOT_TWO = 0.7071067811865476
INV_ROOT_TWOPI = 0.3989422804014327


def offsets_table():
    cells = jnp.arange(WIN * WIN, dtype=jnp.int32)
    rows_at = cells // WIN
    cols_at = cells % WIN
    index_all = (rows_at[:, None] - rows_at[None, :] + WIN - 1) * (2 * WIN - 1) + (
        cols_at[:, None] - cols_at[None, :] + WIN - 1
    )
    entries = jnp.arange((2 * WIN - 1) ** 2, dtype=jnp.int32)
    return (index_all.reshape(-1)[:, None] == entries[None, :]).astype(jnp.float32)


def window_cut(token_grid):
    image_count = token_grid.shape[0]
    tail_dims = token_grid.shape[3:]
    per_side = SIDE // WIN
    token_grid = token_grid.reshape((image_count, per_side, WIN, per_side, WIN) + tail_dims)
    token_grid = jnp.moveaxis(token_grid, 3, 2)
    return token_grid.reshape((image_count * per_side * per_side, WIN * WIN) + tail_dims)


def window_paste(windows, image_count):
    per_side = SIDE // WIN
    tail_dims = windows.shape[2:]
    token_grid = windows.reshape((image_count, per_side, per_side, WIN, WIN) + tail_dims)
    token_grid = jnp.moveaxis(token_grid, 2, 3)
    return token_grid.reshape((image_count, SIDE, SIDE) + tail_dims)


def window_split(token_rows, image_count, shifted):
    token_grid = token_rows.reshape((image_count, SIDE, SIDE) + token_rows.shape[1:])
    if shifted:
        token_grid = jnp.roll(token_grid, (-SHIFT, -SHIFT), (1, 2))
    return window_cut(token_grid)


def window_join(windows, image_count, shifted):
    token_grid = window_paste(windows, image_count)
    if shifted:
        token_grid = jnp.roll(token_grid, (SHIFT, SHIFT), (1, 2))
    return token_grid.reshape((image_count * SIDE * SIDE,) + token_grid.shape[3:])


def region_match():
    line_at = jnp.arange(SIDE, dtype=jnp.int32)
    band_at = jnp.where(line_at < SIDE - WIN, 0, jnp.where(line_at < SIDE - SHIFT, 1, 2))
    region = band_at[:, None] * 3 + band_at[None, :]
    region_win = window_cut(region[None])
    return region_win[:, :, None] == region_win[:, None, :]


def head_bias(offsets, table_vals):
    flat = jnp.dot(offsets, table_vals.T, precision=lax.Precision.HIGHEST)
    return flat.reshape(WIN * WIN, WIN * WIN, -1).transpose(2, 0, 1)


def score_block(query_win, key_win, bias_heads, same_region, image_count, shifted):
    scores = (
        jnp.einsum("wihd,wjhd->whij", query_win, key_win, preferred_element_type=jnp.float32)
        + bias_heads[None]
    )
    if shifted:
        scores = scores.reshape((image_count, -1) + scores.shape[1:])
        scores = jnp.where(same_region[None, :, None], scores, MASKED)
        scores = scores.reshape((-1,) + scores.shape[2:])
    return scores


def normalize(stream):
    centre = stream - jnp.mean(stream, -1, keepdims=True)
    rstd = lax.rsqrt(jnp.mean(centre * centre, -1, keepdims=True) + EPS)
    return (centre * rstd, rstd)


def normalize_back(grad_y, normed, rstd, gain):
    gain_grad = jnp.sum(grad_y * normed, 0)
    shift_grad = jnp.sum(grad_y, 0)
    scaled = grad_y * gain
    grad_x = rstd * (
        scaled
        - jnp.mean(scaled, -1, keepdims=True)
        - normed * jnp.mean(scaled * normed, -1, keepdims=True)
    )
    return (grad_x, gain_grad, shift_grad)


def gelu_slope(pre_act):
    return (
        0.5 * (1.0 + lax.erf(pre_act * INV_ROOT_TWO))
        + pre_act * jnp.exp(-0.5 * pre_act * pre_act) * INV_ROOT_TWOPI
    )


def attend_forward(
    inputs_a, w_mix, mix_bias, table_vals, image_count, shifted, offsets, same_region
):
    local_width = w_mix.shape[2]
    head_count = table_vals.shape[0]
    mixed_qkv = jnp.dot(
        inputs_a, w_mix.reshape(w_mix.shape[0], 3 * local_width), preferred_element_type=jnp.float32
    ).reshape(-1, 3, local_width)
    scale_q = HD ** (-0.5)
    query_rows = ((mixed_qkv[:, 0] + mix_bias[0]) * scale_q).astype(jnp.bfloat16)
    key_rows = mixed_qkv[:, 1].astype(jnp.bfloat16)
    value_rows = (mixed_qkv[:, 2] + mix_bias[1]).astype(jnp.bfloat16)
    query_win = window_split(query_rows.reshape(-1, head_count, HD), image_count, shifted)
    key_win = window_split(key_rows.reshape(-1, head_count, HD), image_count, shifted)
    value_win = window_split(value_rows.reshape(-1, head_count, HD), image_count, shifted)
    bias_heads = head_bias(offsets, table_vals)
    scores = score_block(query_win, key_win, bias_heads, same_region, image_count, shifted)
    row_max = jnp.max(scores, -1, keepdims=True)
    log_total = row_max + jnp.log(jnp.sum(jnp.exp(scores - row_max), -1, keepdims=True))
    probs = jnp.exp(scores - log_total).astype(jnp.bfloat16)
    attended_win = jnp.einsum(
        "whij,wjhd->wihd", probs, value_win, preferred_element_type=jnp.float32
    ).astype(jnp.bfloat16)
    attended = window_join(attended_win, image_count, shifted).reshape(-1, local_width)
    return (attended, (query_win, key_win, value_win, log_total))


def attend_backward(
    att_grad, attn_keep, inputs_a, w_mix, table_vals, image_count, shifted, offsets, same_region
):
    query_win, key_win, value_win, log_total = attn_keep
    local_width = w_mix.shape[2]
    head_count = table_vals.shape[0]
    scale_q = HD ** (-0.5)
    grad_win = window_split(att_grad.reshape(-1, head_count, HD), image_count, shifted)
    bias_heads = head_bias(offsets, table_vals)
    scores = score_block(query_win, key_win, bias_heads, same_region, image_count, shifted)
    probs_f = jnp.exp(scores - log_total)
    probs = probs_f.astype(jnp.bfloat16)
    value_grad = jnp.einsum("whij,wihd->wjhd", probs, grad_win, preferred_element_type=jnp.float32)
    prob_grad = jnp.einsum(
        "wihd,wjhd->whij", grad_win, value_win, preferred_element_type=jnp.float32
    )
    row_dot = jnp.sum(probs_f * prob_grad, -1, keepdims=True)
    score_grad = probs_f * (prob_grad - row_dot)
    table_grad = jnp.dot(
        jnp.sum(score_grad, 0).reshape(head_count, -1), offsets, precision=lax.Precision.HIGHEST
    )
    score_low = score_grad.astype(jnp.bfloat16)
    query_grad = (
        jnp.einsum("whij,wjhd->wihd", score_low, key_win, preferred_element_type=jnp.float32)
        * scale_q
    )
    key_grad = jnp.einsum(
        "whij,wihd->wjhd", score_low, query_win, preferred_element_type=jnp.float32
    )
    query_rows = window_join(query_grad, image_count, shifted).reshape(-1, local_width)
    key_rows = window_join(key_grad, image_count, shifted).reshape(-1, local_width)
    value_rows = window_join(value_grad, image_count, shifted).reshape(-1, local_width)
    mix_bias_grad = jnp.stack([jnp.sum(query_rows, 0), jnp.sum(value_rows, 0)])
    mix_grad = (
        jnp.stack([query_rows, key_rows, value_rows], 1)
        .astype(jnp.bfloat16)
        .reshape(-1, 3 * local_width)
    )
    w_mix_grad = jnp.einsum(
        "td,tk->dk", inputs_a, mix_grad, preferred_element_type=jnp.float32
    ).reshape(w_mix.shape)
    input_grad = jnp.einsum(
        "tk,dk->td", mix_grad, w_mix.reshape(w_mix.shape[0], -1), preferred_element_type=jnp.float32
    )
    return (w_mix_grad, mix_bias_grad, table_grad, input_grad)


def forward_layer(stream, weights, image_count, shifted, offsets, same_region):
    (
        gain_a,
        shift_a,
        w_mix,
        mix_bias,
        table_vals,
        w_out,
        out_bias,
        gain_b,
        shift_b,
        w_up,
        up_bias,
        w_down,
        down_bias,
    ) = weights
    normed_a, rstd_a = normalize(stream)
    inputs_a = (normed_a * gain_a + shift_a).astype(jnp.bfloat16)
    attended, attn_keep = attend_forward(
        inputs_a, w_mix, mix_bias, table_vals, image_count, shifted, offsets, same_region
    )
    branch_a = jnp.dot(attended, w_out, preferred_element_type=jnp.float32)
    branch_a = lax.psum(branch_a.astype(jnp.bfloat16), "mp").astype(jnp.float32)
    middle = stream + branch_a + out_bias
    normed_b, rstd_b = normalize(middle)
    inputs_b = (normed_b * gain_b + shift_b).astype(jnp.bfloat16)
    pre_act = jnp.dot(inputs_b, w_up, preferred_element_type=jnp.float32) + up_bias
    activated = jax.nn.gelu(pre_act, approximate=False).astype(jnp.bfloat16)
    branch_b = jnp.dot(activated, w_down, preferred_element_type=jnp.float32)
    branch_b = lax.psum(branch_b.astype(jnp.bfloat16), "mp").astype(jnp.float32)
    stream_next = middle + branch_b + down_bias
    return (
        stream_next,
        (
            inputs_a,
            normed_a,
            rstd_a,
            attn_keep,
            attended,
            normed_b,
            rstd_b,
            inputs_b,
            pre_act,
            activated,
        ),
    )


def backward_layer(grad_flow, keep, weights, image_count, shifted, offsets, same_region):
    (
        gain_a,
        shift_a,
        w_mix,
        mix_bias,
        table_vals,
        w_out,
        out_bias,
        gain_b,
        shift_b,
        w_up,
        up_bias,
        w_down,
        down_bias,
    ) = weights
    (
        inputs_a,
        normed_a,
        rstd_a,
        attn_keep,
        attended,
        normed_b,
        rstd_b,
        inputs_b,
        pre_act,
        activated,
    ) = keep
    down_bias_grad = jnp.sum(grad_flow, 0)
    grad_low = grad_flow.astype(jnp.bfloat16)
    w_down_grad = jnp.einsum("tf,td->fd", activated, grad_low, preferred_element_type=jnp.float32)
    act_grad = jnp.einsum("td,fd->tf", grad_low, w_down, preferred_element_type=jnp.float32)
    pre_grad = act_grad * gelu_slope(pre_act)
    up_bias_grad = jnp.sum(pre_grad, 0)
    pre_low = pre_grad.astype(jnp.bfloat16)
    w_up_grad = jnp.einsum("td,tf->df", inputs_b, pre_low, preferred_element_type=jnp.float32)
    inputs_b_grad = jnp.einsum("tf,df->td", pre_low, w_up, preferred_element_type=jnp.float32)
    inputs_b_grad = lax.psum(inputs_b_grad.astype(jnp.bfloat16), "mp").astype(jnp.float32)
    mid_grad, gain_b_grad, shift_b_grad = normalize_back(inputs_b_grad, normed_b, rstd_b, gain_b)
    mid_grad = mid_grad + grad_flow
    out_bias_grad = jnp.sum(mid_grad, 0)
    mid_low = mid_grad.astype(jnp.bfloat16)
    w_out_grad = jnp.einsum("tk,td->kd", attended, mid_low, preferred_element_type=jnp.float32)
    att_grad = jnp.einsum("td,kd->tk", mid_low, w_out, preferred_element_type=jnp.float32).astype(
        jnp.bfloat16
    )
    w_mix_grad, mix_bias_grad, table_grad, inputs_a_grad = attend_backward(
        att_grad, attn_keep, inputs_a, w_mix, table_vals, image_count, shifted, offsets, same_region
    )
    inputs_a_grad = lax.psum(inputs_a_grad.astype(jnp.bfloat16), "mp").astype(jnp.float32)
    stream_grad, gain_a_grad, shift_a_grad = normalize_back(inputs_a_grad, normed_a, rstd_a, gain_a)
    stream_grad = stream_grad + mid_grad
    return (
        stream_grad,
        (
            gain_a_grad,
            shift_a_grad,
            w_mix_grad,
            mix_bias_grad,
            table_grad,
            w_out_grad,
            out_bias_grad,
            gain_b_grad,
            shift_b_grad,
            w_up_grad,
            up_bias_grad,
            w_down_grad,
            down_bias_grad,
        ),
    )


def layer_weights(layer_at, matrices, smalls):
    ln1_gain, ln1_bias, qv_bias, rel_table, proj_bias, ln2_gain, ln2_bias, fc1_bias, fc2_bias = (
        smalls
    )
    return (
        ln1_gain[layer_at],
        ln1_bias[layer_at],
        matrices[0][layer_at],
        qv_bias[layer_at],
        rel_table[layer_at],
        matrices[1][layer_at],
        proj_bias[layer_at],
        ln2_gain[layer_at],
        ln2_bias[layer_at],
        matrices[2][layer_at],
        fc1_bias[layer_at],
        matrices[3][layer_at],
        fc2_bias[layer_at],
    )


def per_device(
    images,
    loads,
    cotangent,
    ln1_gain,
    ln1_bias,
    w_qkv,
    qv_bias,
    rel_table,
    w_proj,
    proj_bias,
    ln2_gain,
    ln2_bias,
    w_fc1,
    fc1_bias,
    w_fc2,
    fc2_bias,
):
    slot_count = images.shape[0]
    width_all = images.shape[2]
    offsets = offsets_table()
    same_region = region_match()
    slot_valid = (jnp.arange(slot_count, dtype=jnp.int32) < loads[0]).astype(jnp.float32)
    shards = (w_qkv, w_proj, w_fc1, w_fc2)
    smalls = (
        ln1_gain,
        ln1_bias,
        qv_bias,
        rel_table,
        proj_bias,
        ln2_gain,
        ln2_bias,
        fc1_bias,
        fc2_bias,
    )
    per_micro = slot_count // MICRO
    totals = [[None] * 13 for layer_at in range(LAYERS)]
    outputs = []
    input_grads = []
    for micro_at in range(MICRO):
        lower = micro_at * per_micro
        row_valid = jnp.repeat(slot_valid[lower : lower + per_micro], TOK_IMG)[:, None]
        forward_big = (
            lax.all_gather(shards[0], "dp", axis=1, tiled=True),
            lax.all_gather(shards[1], "dp", axis=2, tiled=True),
            lax.all_gather(shards[2], "dp", axis=1, tiled=True),
            lax.all_gather(shards[3], "dp", axis=2, tiled=True),
        )
        stream = images[lower : lower + per_micro].reshape(-1, width_all).astype(jnp.float32)
        keeps = []
        for layer_at in range(LAYERS):
            weights = layer_weights(layer_at, forward_big, smalls)
            stream, keep = forward_layer(
                stream, weights, per_micro, layer_at % 2 == 1, offsets, same_region
            )
            keeps.append(keep)
        outputs.append(
            (stream * row_valid).astype(jnp.bfloat16).reshape(per_micro, TOK_IMG, width_all)
        )
        backward_big = (
            lax.all_gather(shards[0], "dp", axis=1, tiled=True),
            lax.all_gather(shards[1], "dp", axis=2, tiled=True),
            lax.all_gather(shards[2], "dp", axis=1, tiled=True),
            lax.all_gather(shards[3], "dp", axis=2, tiled=True),
        )
        grad_flow = (
            cotangent[lower : lower + per_micro].reshape(-1, width_all).astype(jnp.float32)
            * row_valid
        )
        for layer_at in reversed(range(LAYERS)):
            weights = layer_weights(layer_at, backward_big, smalls)
            grad_flow, layer_grads = backward_layer(
                grad_flow,
                keeps[layer_at],
                weights,
                per_micro,
                layer_at % 2 == 1,
                offsets,
                same_region,
            )
            for member in range(13):
                if totals[layer_at][member] is None:
                    totals[layer_at][member] = layer_grads[member]
                else:
                    totals[layer_at][member] = totals[layer_at][member] + layer_grads[member]
        input_grads.append(grad_flow.astype(jnp.bfloat16).reshape(per_micro, TOK_IMG, width_all))
    stacked = [
        jnp.stack([totals[layer_at][member] for layer_at in range(LAYERS)]) for member in range(13)
    ]
    result = jnp.concatenate(outputs, 0)
    images_grad = jnp.concatenate(input_grads, 0)
    owned = (
        lax.psum_scatter(stacked[2], "dp", scatter_dimension=1, tiled=True),
        lax.psum_scatter(stacked[5], "dp", scatter_dimension=2, tiled=True),
        lax.psum_scatter(stacked[9], "dp", scatter_dimension=1, tiled=True),
        lax.psum_scatter(stacked[11], "dp", scatter_dimension=2, tiled=True),
    )
    summed = lax.psum(
        (
            stacked[0],
            stacked[1],
            stacked[3],
            stacked[4],
            stacked[6],
            stacked[7],
            stacked[8],
            stacked[10],
            stacked[12],
        ),
        "dp",
    )
    return (
        result,
        images_grad,
        summed[0],
        summed[1],
        owned[0],
        summed[2],
        summed[3],
        owned[1],
        summed[4],
        summed[5],
        summed[6],
        owned[2],
        summed[7],
        owned[3],
        summed[8],
    )


def solution(mesh):
    return jax.shard_map(
        per_device,
        mesh=mesh,
        in_specs=(
            P("dp", None, None),
            P("dp"),
            P("dp", None, None),
            P(),
            P(),
            P(None, "dp", None, "mp"),
            P(None, None, "mp"),
            P(None, "mp", None),
            P(None, "mp", "dp"),
            P(),
            P(),
            P(),
            P(None, "dp", "mp"),
            P(None, "mp"),
            P(None, "mp", "dp"),
            P(),
        ),
        out_specs=(
            P("dp", None, None),
            P("dp", None, None),
            P(),
            P(),
            P(None, "dp", None, "mp"),
            P(None, None, "mp"),
            P(None, "mp", None),
            P(None, "mp", "dp"),
            P(),
            P(),
            P(),
            P(None, "dp", "mp"),
            P(None, "mp"),
            P(None, "mp", "dp"),
            P(),
        ),
        check_vma=False,
    )
```

profile of v0, /device:TPU:0, one launch (start us, length us, event | category | flops | bytes accessed | tf_op | source)
XLA Modules:
  0.0 1123.9 jit_solution(13665094211519431636)
XLA Ops:
  19.2 25.5 %all_gather.9 = bf16[2,256,512]{1,2,0:T(8,128)(2,1)S(1)} all-gather(bf16[2,256,32]{1,2,0:T(8,128)(2,1)S(1)} %copy-done.174), channel_id=1, replica_groups=mesh['dp'=16,'mp'=2] {'dp'}, dimensions={2}, use_global_device_ids=true | all-gather | bytes 557056 | tf_op jit(solution)/shard_map/all_gather | solution.py:372
  44.7 9.4 all-gather.4.cloned.1.call-done
  54.1 5.6 fusion.299
  59.7 3.5 copy.609
  72.8 2.9 fusion.47
  82.1 2.8 fusion.48
  101.5 16.7 %all-reduce.20.cloned.1.call-done = bf16[392,512]{1,0:T(8,128)(2,1)} async-done(((bf16[392,512]{1,0:T(8,128)(2,1)}), bf16[392,512]{1,0:T(8,128)(2,1)}) %all-reduce.20.cloned.1.call-update) | async-done | bytes 401424 | tf_op jit(solution)/shard_map/psum | solution.py:209
  119.8 42.4 %all-gather.6.cloned.1.call-done = bf16[2,512,1024]{2,1,0:T(8,128)(2,1)} async-done(((bf16[2,32,1024]{2,1,0:T(8,128)(2,1)}), bf16[2,512,1024]{2,1,0:T(8,128)(2,1)}) %all-gather.6.cloned.1.call-update) | async-done | bytes 2097168 | tf_op jit(solution)/shard_map/all_gather | solution.py:373
  162.2 6.1 fusion.11
  168.3 36.1 %all-gather.8.cloned.1.call-done = bf16[2,1024,512]{1,2,0:T(8,128)(2,1)} async-done(((bf16[2,1024,32]{1,2,0:T(8,128)(2,1)}), bf16[2,1024,512]{1,2,0:T(8,128)(2,1)}) %all-gather.8.cloned.1.call-update) | async-done | bytes 2097168 | tf_op jit(solution)/shard_map/all_gather | solution.py:374
  204.4 2.7 convolution_convert_fusion.18
  211.0 3.5 copy.610
  214.5 17.5 %all-reduce.22.cloned.1.call-done = bf16[392,512]{1,0:T(8,128)(2,1)} async-done(((bf16[392,512]{1,0:T(8,128)(2,1)}), bf16[392,512]{1,0:T(8,128)(2,1)}) %all-reduce.22.cloned.1.call-update) | async-done | bytes 401424 | tf_op jit(solution)/shard_map/psum | solution.py:216
  267.2 22.9 %all-reduce.24.cloned.1.call-done = bf16[392,512]{1,0:T(8,128)(2,1)} async-done(((bf16[392,512]{1,0:T(8,128)(2,1)}), bf16[392,512]{1,0:T(8,128)(2,1)}) %all-reduce.24.cloned.1.call-update) | async-done | bytes 401424 | tf_op jit(solution)/shard_map/psum | solution.py:209
  303.5 20.4 %all-reduce.32.cloned.1.call-done = bf16[392,512]{1,0:T(8,128)(2,1)} async-done(((bf16[392,512]{1,0:T(8,128)(2,1)}), bf16[392,512]{1,0:T(8,128)(2,1)}) %all-reduce.32.cloned.1.call-update) | async-done | bytes 401424 | tf_op jit(solution)/shard_map/psum | solution.py:272
  336.0 3.1 copy.523
  359.5 25.8 %all-reduce.34.cloned.1.call-done = bf16[392,512]{1,0:T(8,128)(2,1)} async-done(((bf16[392,512]{1,0:T(8,128)(2,1)}), bf16[392,512]{1,0:T(8,128)(2,1)}) %all-reduce.34.cloned.1.call-update) | async-done | bytes 401424 | tf_op jit(solution)/shard_map/psum | solution.py:284
  401.8 18.1 %all-reduce.36.cloned.1.call-done = bf16[392,512]{1,0:T(8,128)(2,1)} async-done(((bf16[392,512]{1,0:T(8,128)(2,1)}), bf16[392,512]{1,0:T(8,128)(2,1)}) %all-reduce.36.cloned.1.call-update) | async-done | bytes 401424 | tf_op jit(solution)/shard_map/psum | solution.py:272
  430.2 2.9 multiply_reduce_fusion.2
  452.8 16.2 %all-reduce.26.cloned.1.call-done = bf16[392,512]{1,0:T(8,128)(2,1)} async-done(((bf16[392,512]{1,0:T(8,128)(2,1)}), bf16[392,512]{1,0:T(8,128)(2,1)}) %all-reduce.26.cloned.1.call-update) | async-done | bytes 401424 | tf_op jit(solution)/shard_map/psum | solution.py:209
  470.8 4.9 fusion.17
  480.1 3.3 fusion.251
  483.4 20.8 %all-reduce.28.cloned.1.call-done = bf16[392,512]{1,0:T(8,128)(2,1)} async-done(((bf16[392,512]{1,0:T(8,128)(2,1)}), bf16[392,512]{1,0:T(8,128)(2,1)}) %all-reduce.28.cloned.1.call-update) | async-done | bytes 401424 | tf_op jit(solution)/shard_map/psum | solution.py:216
  542.9 2.9 fusion.88
  555.6 3.2 convolution_bitcast_fusion.4
  558.8 3.1 copy.541
  566.7 2.7 convolution_bitcast_fusion.5
  576.4 5.1 all-reduce.30.cloned.1.call-done
  583.1 9.5 fusion.14
  599.5 3.0 copy.533
  609.5 13.6 %all-reduce.38.cloned.1.call-done = bf16[392,512]{1,0:T(8,128)(2,1)} async-done(((bf16[392,512]{1,0:T(8,128)(2,1)}), bf16[392,512]{1,0:T(8,128)(2,1)}) %all-reduce.38.cloned.1.call-update) | async-done | bytes 401424 | tf_op jit(solution)/shard_map/psum | solution.py:272
  637.7 3.3 convolution_bitcast_fusion.2
  641.0 3.1 copy.558
  658.0 3.1 copy.550
  668.5 3.3 stack_reshape_reshape.28
  674.1 3.1 stack_reshape_reshape.27
  679.4 3.1 stack_reshape_reshape.29
  682.5 2.8 maximum_convert_fusion.1
  692.7 21.3 %all-reduce.40.cloned.1.call-done = bf16[392,512]{1,0:T(8,128)(2,1)} async-done(((bf16[392,512]{1,0:T(8,128)(2,1)}), bf16[392,512]{1,0:T(8,128)(2,1)}) %all-reduce.40.cloned.1.call-update) | async-done | bytes 401424 | tf_op jit(solution)/shard_map/psum | solution.py:284
  718.2 3.4 fusion.318
  724.2 3.0 convolution_convert_fusion.16
  728.6 21.5 %all-reduce.42.cloned.1.call-done = bf16[392,512]{1,0:T(8,128)(2,1)} async-done(((bf16[392,512]{1,0:T(8,128)(2,1)}), bf16[392,512]{1,0:T(8,128)(2,1)}) %all-reduce.42.cloned.1.call-update) | async-done | bytes 401424 | tf_op jit(solution)/shard_map/psum | solution.py:272
  763.6 2.8 convolution_bitcast_fusion
  798.0 7.5 copy.588
  876.1 62.8 %all-reduce.2 = (f32[2,512]{1,0:T(2,128)}, f32[2,512]{1,0:T(2,128)}, f32[2,2,256]{2,1,0:T(2,128)}, f32[2,8,169]{2,1,0:T(8,128)}, f32[2,512]{1,0:T(2,128)}, /*ind...) all-reduce(f32[2,512]{1,0:T(2,128)S(1)} %pad_maximum_fusion.36, ...), channel_id=1, replica_groups=mesh['dp'=16,'mp'=2] {'dp'}, use_global_device_ids=true, to_apply=%region_64.65 | all-reduce | flops 11920 | bytes 95360 | tf_op jit(solution)/shard_map/psum | solution.py:425
  938.8 31.8 %all-reduce.44.cloned.1.call-done = (f32[2,256,512]{1,0,2:T(2,128)}, f32[2,1024,512]{1,0,2:T(2,128)}) async-done(((f32[2,256,512]{1,0,2:T(2,128)}, f32[2,1024,512]{1,0,2:T(2,128)}), (f32[2,256,512]{1,0,2:T(2,128)}, f32[2,1024,512]{1,0,2:T(2,128)})) %all-reduce.44.cloned.1.call-update) | async-done | bytes 5242896
  973.9 67.2 %reduce-scatter.3.cloned.1.call-done = f32[2,32,3,256]{3,1,2,0:T(8,128)} async-done(((f32[2,512,3,256]{3,1,2,0:T(8,128)}), f32[2,32,3,256]{3,1,2,0:T(8,128)}) %reduce-scatter.3.cloned.1.call-update) | async-done | bytes 196624 | tf_op jit(solution)/shard_map/reduce_scatter | solution.py:420
  1041.1 76.1 %reduce-scatter.5.cloned.1.call-done = f32[2,32,1024]{2,1,0:T(8,128)} async-done(((f32[2,512,1024]{2,1,0:T(8,128)}), f32[2,32,1024]{2,1,0:T(8,128)}) %reduce-scatter.5.cloned.1.call-update) | async-done | bytes 262160 | tf_op jit(solution)/shard_map/reduce_scatter | solution.py:422
  (971 shorter events, 429.7 us)
Async XLA Ops:
  7.2 46.9 %all-gather.4.cloned.1.call-start = ((), (), s32[]{:S(2)}) async-start(), calls=%async_computation.2 | async-start | bytes 1671168 | tf_op jit(solution)/shard_map/all_gather | solution.py:371
  9.0 109.3 %all-reduce.20.cloned.1.call-start = ((), (), s32[]{:S(2)}) async-start(), calls=%async_computation.3 | async-start | bytes 802816 | tf_op jit(solution)/shard_map/psum | solution.py:209
  9.2 90.4 %copy-start.152 = (s32[49,49]{1,0:T(8,128)}, s32[49,49]{1,0:T(8,128)S(1)}, u32[]{:S(2)}) copy-start(s32[49,49]{1,0:T(8,128)S(1)} %add_add_fusion.6) | copy-start | bytes 28816
  12.9 75.0 %copy-start.12 = (f32[8,49,49]{1,2,0:T(8,128)}, f32[8,49,49]{1,2,0:T(8,128)S(1)}, u32[]{:S(2)}) copy-start(f32[8,49,49]{1,2,0:T(8,128)S(1)} %copy.469) | copy-start | bytes 230500
  13.0 493.0 %copy-start.150 = (f32[1,512]{1,0:T(1,128)}, f32[1,512]{1,0:T(1,128)S(1)}, u32[]{:S(2)}) copy-start(f32[1,512]{1,0:T(1,128)S(1)} %get-tuple-element.226) | copy-start | bytes 6148
  18.6 44.6 %copy-start.112 = (bf16[392,512,1]{1,0,2:T(8,128)(2,1)}, bf16[392,512,1]{1,0,2:T(8,128)(2,1)S(1)}, u32[]{:S(2)}) copy-start(bf16[392,512,1]{1,0,2:T(8,128)(2,1)S(1)} %reshape.1284) | copy-start | bytes 1204228
  19.2 45.4 %copy-start.85 = (bf16[392,512,1]{1,0,2:T(8,128)(2,1)}, bf16[392,512,1]{1,0,2:T(8,128)(2,1)S(1)}, u32[]{:S(2)}) copy-start(bf16[392,512,1]{1,0,2:T(8,128)(2,1)S(1)} %reshape.1288) | copy-start | bytes 1204228
  44.7 218.0 %copy-start.22 = (bf16[2,256,512]{1,2,0:T(8,128)(2,1)}, bf16[2,256,512]{1,2,0:T(8,128)(2,1)S(1)}, u32[]{:S(2)}) copy-start(bf16[2,256,512]{1,2,0:T(8,128)(2,1)S(1)} %all_gather.9) | copy-start | bytes 1572868
  93.4 68.8 %all-gather.6.cloned.1.call-start = ((), (), s32[]{:S(2)}) async-start(), calls=%async_computation.4 | async-start | bytes 2228224 | tf_op jit(solution)/shard_map/all_gather | solution.py:373
  94.1 110.3 %all-gather.8.cloned.1.call-start = ((), (), s32[]{:S(2)}) async-start(), calls=%async_computation.5 | async-start | bytes 2228224 | tf_op jit(solution)/shard_map/all_gather | solution.py:374
  94.7 137.3 %all-reduce.22.cloned.1.call-start = ((), (), s32[]{:S(2)}) async-start(), calls=%async_computation.6 | async-start | bytes 802816 | tf_op jit(solution)/shard_map/psum | solution.py:216
  98.2 227.9 %copy-start.154 = (f32[1,512]{1,0:T(1,128)}, f32[1,512]{1,0:T(1,128)S(1)}, u32[]{:S(2)}) copy-start(f32[1,512]{1,0:T(1,128)S(1)} %get-tuple-element.222) | copy-start | bytes 6148
  98.2 372.4 %copy-start.158 = (f32[1,512]{1,0:T(1,128)}, f32[1,512]{1,0:T(1,128)S(1)}, u32[]{:S(2)}) copy-start(f32[1,512]{1,0:T(1,128)S(1)} %get-tuple-element.223) | copy-start | bytes 6148
  98.9 63.3 %copy-start.207 = (f32[1,512]{1,0:T(1,128)}, f32[1,512]{1,0:T(1,128)S(1)}, u32[]{:S(2)}) copy-start(f32[1,512]{1,0:T(1,128)S(1)} %get-tuple-element.225) | copy-start | bytes 6148
  99.5 62.7 %copy-start.233 = (f32[1,1024]{1,0:T(1,128)}, f32[1,1024]{1,0:T(1,128)S(1)}, u32[]{:S(2)}) copy-start(f32[1,1024]{1,0:T(1,128)S(1)} %get-tuple-element.217) | copy-start | bytes 12292
  119.5 112.6 %copy-start.15 = (f32[392,512]{1,0:T(8,128)}, f32[392,512]{1,0:T(8,128)S(1)}, u32[]{:S(2)}) copy-start(f32[392,512]{1,0:T(8,128)S(1)} %get-tuple-element.194) | copy-start | bytes 2408452
  119.5 302.5 %copy-start.177 = (f32[392]{0:T(512)}, f32[392]{0:T(512)S(1)}, u32[]{:S(2)}) copy-start(f32[392]{0:T(512)S(1)} %broadcast_multiply_fusion.23) | copy-start | bytes 4708
  119.8 302.2 %copy-start.187 = (f32[392]{0:T(512)}, f32[392]{0:T(512)S(1)}, u32[]{:S(2)}) copy-start(f32[392]{0:T(512)S(1)} %add_rsqrt_fusion.7) | copy-start | bytes 4708
  168.3 38.9 %copy-start.127 = (bf16[392,1024]{1,0:T(8,128)(2,1)}, bf16[392,1024]{1,0:T(8,128)(2,1)S(1)}, u32[]{:S(2)}) copy-start(bf16[392,1024]{1,0:T(8,128)(2,1)S(1)} %get-tuple-element.243) | copy-start | bytes 2408452
  207.2 82.9 %all-reduce.24.cloned.1.call-start = ((), (), s32[]{:S(2)}) async-start(), calls=%async_computation.7 | async-start | bytes 802816 | tf_op jit(solution)/shard_map/psum | solution.py:209
  209.0 42.9 %copy-start.100 = (f32[8,49,49]{1,2,0:T(8,128)}, f32[8,49,49]{1,2,0:T(8,128)S(1)}, u32[]{:S(2)}) copy-start(f32[8,49,49]{1,2,0:T(8,128)S(1)} %copy.480) | copy-start | bytes 230500
  233.2 154.3 %copy-start.166 = (f32[392]{0:T(512)}, f32[392]{0:T(512)S(1)}, u32[]{:S(2)}) copy-start(f32[392]{0:T(512)S(1)} %broadcast_multiply_fusion.22) | copy-start | bytes 4708
  233.5 154.0 %copy-start.185 = (f32[392]{0:T(512)}, f32[392]{0:T(512)S(1)}, u32[]{:S(2)}) copy-start(f32[392]{0:T(512)S(1)} %add_rsqrt_fusion.6) | copy-start | bytes 4708
  262.7 27.4 %copy-start.104 = (bf16[392,256]{1,0:T(8,128)(2,1)}, bf16[392,256]{1,0:T(8,128)(2,1)S(1)}, u32[]{:S(2)}) copy-start(bf16[392,256]{1,0:T(8,128)(2,1)S(1)} %reshape_reshape.8) | copy-start | bytes 602116
  262.7 27.4 %copy-start.192 = (f32[1,512]{1,0:T(1,128)S(1)}, f32[1,512]{1,0:T(1,128)}, u32[]{:S(2)}) copy-start(f32[1,512]{1,0:T(1,128)} %get-tuple-element.235) | copy-start | bytes 6148
  263.8 60.2 %all-reduce.32.cloned.1.call-start = ((), (), s32[]{:S(2)}) async-start(), calls=%async_computation.11 | async-start | bytes 802816 | tf_op jit(solution)/shard_map/psum | solution.py:272
  264.5 26.9 %copy-start.223 = (f32[2]{0:T(128)}, f32[2]{0:T(128)S(1)}, u32[]{:S(2)}) copy-start(f32[2]{0:T(128)S(1)} %get-tuple-element.240) | copy-start | bytes 28
  291.5 34.6 %copy-start.4 = (f32[392,512]{1,0:T(8,128)}, f32[392,512]{1,0:T(8,128)S(1)}, u32[]{:S(2)}) copy-start(f32[392,512]{1,0:T(8,128)S(1)} %get-tuple-element.190) | copy-start | bytes 2408452
  291.5 34.6 %copy-start.162 = (f32[392]{0:T(512)}, f32[392]{0:T(512)S(1)}, u32[]{:S(2)}) copy-start(f32[392]{0:T(512)S(1)} %broadcast_multiply_fusion.21) | copy-start | bytes 4708
  291.7 34.4 %copy-start.181 = (f32[392]{0:T(512)}, f32[392]{0:T(512)S(1)}, u32[]{:S(2)}) copy-start(f32[392]{0:T(512)S(1)} %add_rsqrt_fusion.5) | copy-start | bytes 4708
  297.7 87.6 %all-reduce.34.cloned.1.call-start = ((), (), s32[]{:S(2)}) async-start(), calls=%async_computation.12 | async-start | bytes 802816 | tf_op jit(solution)/shard_map/psum | solution.py:284
  299.4 26.8 %copy-start.175 = (f32[392]{0:T(512)}, f32[392]{0:T(512)S(1)}, u32[]{:S(2)}) copy-start(f32[392]{0:T(512)S(1)} %mul.673) | copy-start | bytes 4708
  357.7 29.8 %copy-start.33 = (f32[392,512]{1,0:T(8,128)S(1)}, f32[392,512]{1,0:T(8,128)}, u32[]{:S(2)}) copy-start(f32[392,512]{1,0:T(8,128)} %copy-done.32) | copy-start | bytes 2408452
  359.0 60.8 %all-reduce.36.cloned.1.call-start = ((), (), s32[]{:S(2)}) async-start(), calls=%async_computation.13 | async-start | bytes 802816 | tf_op jit(solution)/shard_map/psum | solution.py:272
  393.5 75.5 %all-reduce.26.cloned.1.call-start = ((), (), s32[]{:S(2)}) async-start(), calls=%async_computation.8 | async-start | bytes 802816 | tf_op jit(solution)/shard_map/psum | solution.py:209
  442.8 61.4 %all-reduce.28.cloned.1.call-start = ((), (), s32[]{:S(2)}) async-start(), calls=%async_computation.9 | async-start | bytes 802816 | tf_op jit(solution)/shard_map/psum | solution.py:216
  477.9 103.5 %all-reduce.30.cloned.1.call-start = ((), (), s32[]{:S(2)}) async-start(), calls=%async_computation.10 | async-start | bytes 802816 | tf_op jit(solution)/shard_map/psum | solution.py:209
  555.1 67.9 %all-reduce.38.cloned.1.call-start = ((), (), s32[]{:S(2)}) async-start(), calls=%async_computation.14 | async-start | bytes 802816 | tf_op jit(solution)/shard_map/psum | solution.py:272
  582.7 42.7 %copy-start.160 = (f32[392]{0:T(512)}, f32[392]{0:T(512)S(1)}, u32[]{:S(2)}) copy-start(f32[392]{0:T(512)S(1)} %broadcast_multiply_fusion.18) | copy-start | bytes 4708
  583.1 42.4 %copy-start.172 = (f32[392]{0:T(512)}, f32[392]{0:T(512)S(1)}, u32[]{:S(2)}) copy-start(f32[392]{0:T(512)S(1)} %add_rsqrt_fusion.2) | copy-start | bytes 4708
  596.8 117.2 %all-reduce.40.cloned.1.call-start = ((), (), s32[]{:S(2)}) async-start(), calls=%async_computation.15 | async-start | bytes 802816 | tf_op jit(solution)/shard_map/psum | solution.py:284
  687.6 26.3 %copy-start.151 = (f32[1,512]{1,0:T(1,128)S(1)}, f32[1,512]{1,0:T(1,128)}, u32[]{:S(2)}) copy-start(f32[1,512]{1,0:T(1,128)} %copy-done.150) | copy-start | bytes 6148
  687.6 26.3 %copy-start.157 = (f32[392]{0:T(512)S(1)}, f32[392]{0:T(512)}, u32[]{:S(2)}) copy-start(f32[392]{0:T(512)} %copy-done.156) | copy-start | bytes 4708
  687.7 62.5 %all-reduce.42.cloned.1.call-start = ((), (), s32[]{:S(2)}) async-start(), calls=%async_computation.16 | async-start | bytes 802816 | tf_op jit(solution)/shard_map/psum | solution.py:272
  723.9 141.4 %all-reduce.46.cloned.1.call-start = ((), (), s32[]{:S(2)}) async-start(), calls=%async_computation.20 | async-start | bytes 3211264 | tf_op jit(solution)/shard_map/psum | solution.py:216
  789.1 181.6 %all-reduce.44.cloned.1.call-start = ((), (), s32[]{:S(2)}) async-start(), calls=%async_computation.19 | async-start | bytes 10485760
  807.9 233.2 %reduce-scatter.3.cloned.1.call-start = ((), (), s32[]{:S(2)}) async-start(), calls=%async_computation.17 | async-start | bytes 3342336 | tf_op jit(solution)/shard_map/reduce_scatter | solution.py:420
  816.0 301.2 %reduce-scatter.5.cloned.1.call-start = ((), (), s32[]{:S(2)}) async-start(), calls=%async_computation.18 | async-start | bytes 4456448 | tf_op jit(solution)/shard_map/reduce_scatter | solution.py:422
  (223 other events, 911.1 us)
Sparse Core Ops, SparseCore 0:
  10.9 43.1 all-gather.3
  93.5 24.7 all-reduce.19
  120.5 41.6 all-gather.5
  164.2 40.1 all-gather.7
  207.3 24.6 all-reduce.21
  263.9 26.1 all-reduce.23
  297.8 26.1 all-reduce.31
  359.1 26.1 all-reduce.33
  393.6 26.1 all-reduce.35
  442.9 26.1 all-reduce.25
  478.0 26.1 all-reduce.27
  555.2 26.1 all-reduce.29
  596.9 26.1 all-reduce.37
  687.8 26.1 all-reduce.39
  724.0 26.1 all-reduce.41
  789.2 52.4 all-reduce.45
  845.3 125.2 all-reduce.43
  974.9 66.1 reduce-scatter.2
  1045.5 71.6 reduce-scatter.4
where the time goes:
time: 1130 us; the launch traced here: 1120 us
  waiting for transfers between devices  485 us (43%)
  local copies, waits for them, and re-layouts  266 us (24%)
  matrix products  134 us (12%)
  other arithmetic  129 us (11%)
  blocking collectives  88.3 us (8%)
  between operations  18.7 us (2%)
    reduce_scatter x1, waiting for transfers between devices, per_device(): lax.psum_scatter(stacked[9], 'dp', scatter_dimension=1, tiled=True)  76.1 us
    psum x4, waiting for transfers between devices, backward_layer(): lax.psum(inputs_b_grad.astype(jnp.bfloat16), 'mp').astype(jnp.float32)  73.6 us
    reduce_scatter x1, waiting for transfers between devices, per_device(): lax.psum_scatter(stacked[2], 'dp', scatter_dimension=1, tiled=True)  67.2 us
    psum x1, blocking collectives, per_device(): lax.psum((stacked[0], stacked[1], stacked[3], stacked[4], stacked[6], sta...  62.8 us
    psum x4, waiting for transfers between devices, forward_layer(): branch_a = lax.psum(branch_a.astype(jnp.bfloat16), 'mp').astype(jnp.float32)  60.9 us
    psum x2, waiting for transfers between devices, backward_layer(): lax.psum(inputs_a_grad.astype(jnp.bfloat16), 'mp').astype(jnp.float32)  47.1 us
    unnamed x520, local copies, waits for them, and re-layouts  43.5 us
    all_gather x1, waiting for transfers between devices, per_device(): lax.all_gather(shards[2], 'dp', axis=1, tiled=True)  42.4 us
  transfers between devices with their start and end apart: 19, of which 18 were waited for; matrix products, arithmetic and copies ran while one was open for 16% of the time, Pallas kernels for 0%

commit v1 on v0

v1 whole, which is shorter than its diff:
```python
import functools
import types

import jax
import jax.numpy as jnp
import numpy as np
from jax import lax
from jax.experimental import pallas as pl
from jax.experimental.pallas import tpu as pltpu
from jax.sharding import PartitionSpec as P

D = 512
HD = 32
FF = 2048
SIDE = 14
WIN = 7
SHIFT = 3
LAYERS = 2
TOK_IMG = SIDE * SIDE
CELLS = WIN * WIN
PADC = 64
EPS = 1e-05
MASKED = -1e30
INV_ROOT_TWO = 0.7071067811865476
INV_ROOT_TWOPI = 0.3989422804014327
SCALE_Q = HD**-0.5

OWN = 2
ROWS = 400
WROWS = OWN * 4 * PADC
STEP = 80
HALF = 256
F32 = jnp.float32
BF16 = jnp.bfloat16


def token_maps():
    idx = np.full((LAYERS, WROWS), -1, np.int32)
    reg = np.zeros((LAYERS, 4, PADC), np.int32)
    for layer in range(LAYERS):
        shift = SHIFT if layer % 2 else 0
        for win in range(OWN * 4):
            img, wr, wc = win // 4, (win // 2) % 2, win % 2
            for cell in range(CELLS):
                r, c = wr * WIN + cell // WIN, wc * WIN + cell % WIN
                idx[layer, win * PADC + cell] = (
                    img * TOK_IMG + ((r + shift) % SIDE) * SIDE + (c + shift) % SIDE
                )
                if shift:
                    band = lambda v: 0 if v < SIDE - WIN else (1 if v < SIDE - SHIFT else 2)
                    reg[layer, win % 4, cell] = 3 * band(r) + band(c)
    return idx, reg


def bias_onehot():
    cells = np.arange(CELLS)
    r, c = cells // WIN, cells % WIN
    entry = (r[None, :] - r[:, None] + WIN - 1) * (2 * WIN - 1) + (
        c[None, :] - c[:, None] + WIN - 1
    )
    full = np.full((PADC, PADC), -1, np.int32)
    full[:CELLS, :CELLS] = entry
    return full


def dot(a, b):
    return jnp.dot(a, b, preferred_element_type=F32)


def dot_nt(a, b):
    return lax.dot_general(a, b, (((1,), (1,)), ((), ())), preferred_element_type=F32)


def dot_tn(a, b):
    return lax.dot_general(a, b, (((0,), (0,)), ((), ())), preferred_element_type=F32)


def lane_head(shape):
    return lax.broadcasted_iota(jnp.int32, shape, 1) // HD


def spread_heads(block):
    head = lane_head(block.shape)
    zero = jnp.zeros_like(block)
    return jnp.concatenate([jnp.where(head == h, block, zero) for h in range(4)], axis=0)


def gather_heads(stack):
    head = lane_head((PADC, 128))
    total = jnp.where(head == 0, stack[:PADC], 0.0)
    for h in range(1, 4):
        total = total + jnp.where(head == h, stack[h * PADC : (h + 1) * PADC], 0.0)
    return total


def row_loop(body, init):
    def step(i, carry):
        return body(pl.ds(pl.multiple_of(i * STEP, STEP), STEP), carry)

    return lax.fori_loop(0, ROWS // STEP, step, init)


def weight(r, l, g, x, cols):
    part = r.W[l, g, x, :, :, cols]
    return part.reshape(D, part.shape[-1])


def weight_rows(r, l, g, x, n, cols):
    per = HALF // r.W.shape[4]
    part = r.W[l, g, x, pl.ds(n * per, per), :, cols]
    return part.reshape(HALF, part.shape[-1])


def put_grad(r, l, g, x, cols, value):
    z, rb = r.G.shape[3], r.G.shape[4]
    r.G[l, g, x, :, :, cols] = value.astype(BF16).reshape(z, rb, value.shape[-1])


def norm_into(r, l, src, normed, rstd_ref, gain, shift, out):
    def body(rows, carry):
        s = src[rows, :]
        centre = s - jnp.mean(s, -1, keepdims=True)
        rstd = lax.rsqrt(jnp.mean(centre * centre, -1, keepdims=True) + EPS)
        n = centre * rstd
        normed[l, rows, :] = n
        rstd_ref[l, rows, :] = rstd
        out[rows, :] = (n * gain[l] + shift[l]).astype(BF16)
        return carry

    row_loop(body, 0)


def norm_back(r, l, grad_y, normed, rstd_ref, gain, base, out, out_low):
    def body(rows, carry):
        gain_sum, shift_sum, out_sum = carry
        gy = grad_y[rows, :]
        n = normed[l, rows, :]
        e = gy * gain[l]
        back = rstd_ref[l, rows, :] * (
            e - jnp.mean(e, -1, keepdims=True) - n * jnp.mean(e * n, -1, keepdims=True)
        )
        res = base[rows, :] + back
        out[rows, :] = res
        out_low[rows, :] = res.astype(BF16)
        return (
            gain_sum + jnp.sum(gy * n, 0, keepdims=True),
            shift_sum + jnp.sum(gy, 0, keepdims=True),
            out_sum + jnp.sum(res, 0, keepdims=True),
        )

    zero = jnp.zeros((1, D), F32)
    return row_loop(body, (zero, zero, zero))


def to_windows(r, l):
    tok = lax.broadcasted_iota(jnp.int32, (WROWS, ROWS), 1)
    return jnp.where(tok == r.idx_col[l], 1.0, 0.0).astype(BF16)


def to_grid(r, l):
    tok = lax.broadcasted_iota(jnp.int32, (ROWS, WROWS), 0)
    return jnp.where(tok == r.idx_row[l], 1.0, 0.0).astype(BF16)


def attention_forward(r, l):
    def window(w, carry):
        rows = pl.ds(pl.multiple_of(w * PADC, PADC), PADC)
        pos = lax.rem(w, 4)
        same = r.reg_col[l, pos] == r.reg_row[l, pos]
        for g in range(4):
            lanes = slice(g * 128, (g + 1) * 128)
            q, k, v = r.Q[l, rows, lanes], r.K[l, rows, lanes], r.V[l, rows, lanes]
            s = dot_nt(k, spread_heads(q)) + r.bias[l, g]
            s = jnp.where(same, s, MASKED)
            e = jnp.exp(s - jnp.max(s, 0, keepdims=True))
            p = (e / jnp.sum(e, 0, keepdims=True)).astype(BF16)
            r.PR[l, w * 4 + g] = p
            r.AW[rows, lanes] = gather_heads(dot_tn(p, v)).astype(BF16)
        return carry

    lax.fori_loop(0, OWN * 4, window, 0)


def attention_backward(r, l):
    zero = jnp.zeros((1, 128), F32)

    def window(w, carry):
        rows = pl.ds(pl.multiple_of(w * PADC, PADC), PADC)
        sums = list(carry)
        for g in range(4):
            lanes = slice(g * 128, (g + 1) * 128)
            q, k, v = r.Q[l, rows, lanes], r.K[l, rows, lanes], r.V[l, rows, lanes]
            da = r.AW[rows, lanes]
            p = r.PR[l, w * 4 + g]
            da_spread = spread_heads(da)
            pf = p.astype(F32)
            pg = dot_nt(v, da_spread)
            ds = pf * (pg - jnp.sum(pf * pg, 0, keepdims=True))
            r.DS[l, g] += ds
            low = ds.astype(BF16)
            dv = dot(p, da_spread)
            dk = dot(low, spread_heads(q))
            dq = gather_heads(dot_tn(low, k)) * SCALE_Q
            x, at = g // 2, (g % 2) * 128
            r.DM[x, rows, at : at + 128] = dq.astype(BF16)
            r.DM[x, rows, HALF + at : HALF + at + 128] = dk.astype(BF16)
            r.DM[x, rows, 2 * HALF + at : 2 * HALF + at + 128] = dv.astype(BF16)
            sums[g] = sums[g] + jnp.sum(dq, 0, keepdims=True)
            sums[4 + g] = sums[4 + g] + jnp.sum(dv, 0, keepdims=True)
        return tuple(sums)

    return lax.fori_loop(0, OWN * 4, window, (zero,) * 8)


def forward(r, l):
    norm_into(r, l, r.S, r.N1, r.R1, r.ln1_gain, r.ln1_bias, r.YB)
    r.YW[l] = dot(to_windows(r, l), r.YB[...]).astype(BF16)
    yw = r.YW[l]
    for x in range(2):
        cols = slice(x * HALF, (x + 1) * HALF)
        q = dot(yw, weight(r, l, 0, x, slice(0, HALF)))
        r.Q[l, :, cols] = ((q + r.qv_bias[l, 0:1, cols]) * SCALE_Q).astype(BF16)
        r.K[l, :, cols] = dot(yw, weight(r, l, 0, x, slice(HALF, 2 * HALF))).astype(BF16)
        v = dot(yw, weight(r, l, 0, x, slice(2 * HALF, 3 * HALF)))
        r.V[l, :, cols] = (v + r.qv_bias[l, 1:2, cols]).astype(BF16)
    attention_forward(r, l)
    r.AT[l] = dot(to_grid(r, l), r.AW[...]).astype(BF16)
    for n in range(2):
        cols = slice(n * HALF, (n + 1) * HALF)
        acc = dot_nt(r.AT[l, :, :HALF], weight_rows(r, l, 0, 0, n, slice(3 * HALF, 4 * HALF)))
        acc += dot_nt(r.AT[l, :, HALF:], weight_rows(r, l, 0, 1, n, slice(3 * HALF, 4 * HALF)))
        r.S[:, cols] = r.S[:, cols] + acc + r.proj_bias[l, :, cols]
    norm_into(r, l, r.S, r.N2, r.R2, r.ln2_gain, r.ln2_bias, r.YB)
    r.Y2[l] = r.YB[...]
    for x in range(2):

        def up(n, carry):
            at = pl.ds(pl.multiple_of(n * HALF, HALF), HALF)
            full = pl.ds(pl.multiple_of(x * 1024 + n * HALF, HALF), HALF)
            pre = dot(r.YB[...], weight(r, l, 1, x, at)) + r.fc1_bias[l, :, full]
            phi = 0.5 * (1.0 + lax.erf(pre * INV_ROOT_TWO))
            r.AC[l, :, full] = (pre * phi).astype(BF16)
            dens = jnp.exp(-0.5 * pre * pre) * INV_ROOT_TWOPI
            r.SL[l, :, full] = (phi + pre * dens).astype(BF16)
            return carry

        lax.fori_loop(0, 4, up, 0)
    for n in range(2):
        cols = slice(n * HALF, (n + 1) * HALF)
        acc = dot_nt(r.AC[l, :, :1024], weight_rows(r, l, 2, 0, n, slice(0, 1024)))
        acc += dot_nt(r.AC[l, :, 1024:], weight_rows(r, l, 2, 1, n, slice(0, 1024)))
        r.S[:, cols] = r.S[:, cols] + acc + r.fc2_bias[l, :, cols]


def backward_mlp(r, l):
    def low(rows, total):
        g = r.S[rows, :]
        r.YB[rows, :] = g.astype(BF16)
        return total + jnp.sum(g, 0, keepdims=True)

    r.SG[l, 2:3, D : 2 * D] = row_loop(low, jnp.zeros((1, D), F32))
    r.TA[...] = r.YB[...].T
    r.TB[...] = r.Y2[l].T
    for x in range(2):

        def down(n, carry):
            at = pl.ds(pl.multiple_of(n * HALF, HALF), HALF)
            full = pl.ds(pl.multiple_of(x * 1024 + n * HALF, HALF), HALF)
            pg = dot(r.YB[...], weight(r, l, 2, x, at)) * r.SL[l, :, full].astype(F32)
            r.SG[l, 0:1, full] = jnp.sum(pg, 0, keepdims=True)
            pb = pg.astype(BF16)
            r.PB[:, full] = pb
            put_grad(r, l, 2, x, at, dot(r.TA[...], r.AC[l, :, full]))
            put_grad(r, l, 1, x, at, dot(r.TB[...], pb))
            return carry

        lax.fori_loop(0, 4, down, 0)
    for n in range(2):
        cols = slice(n * HALF, (n + 1) * HALF)
        acc = dot_nt(r.PB[:, :1024], weight_rows(r, l, 1, 0, n, slice(0, 1024)))
        acc += dot_nt(r.PB[:, 1024:], weight_rows(r, l, 1, 1, n, slice(0, 1024)))
        r.GY[:, cols] = acc
    gain, shift, out = norm_back(r, l, r.GY, r.N2, r.R2, r.ln2_gain, r.S, r.S, r.YB)
    r.SG[l, 1:2, 2 * D : 3 * D] = gain
    r.SG[l, 1:2, 3 * D :] = shift
    r.SG[l, 2:3, :D] = out


def backward_attention(r, l):
    r.TA[...] = r.YB[...].T
    for x in range(2):
        cols = slice(x * HALF, (x + 1) * HALF)
        put_grad(r, l, 0, x, slice(3 * HALF, 4 * HALF), dot(r.TA[...], r.AT[l, :, cols]))
        att = dot(r.YB[...], weight(r, l, 0, x, slice(3 * HALF, 4 * HALF)))
        r.GB[:, cols] = att.astype(BF16)
    r.AW[...] = dot(to_windows(r, l), r.GB[...]).astype(BF16)
    r.DS[l] = jnp.zeros_like(r.DS[l])
    sums = attention_backward(r, l)
    for g in range(4):
        r.SG[l, 2:3, 2 * D + g * 128 : 2 * D + (g + 1) * 128] = sums[g]
        r.SG[l, 2:3, 3 * D + g * 128 : 3 * D + (g + 1) * 128] = sums[4 + g]
    r.TW[...] = r.YW[l].T
    for x in range(2):
        for part in range(3):
            cols = slice(part * HALF, (part + 1) * HALF)
            put_grad(r, l, 0, x, cols, dot(r.TW[...], r.DM[x, :, cols]))
    for n in range(2):
        cols = slice(n * HALF, (n + 1) * HALF)
        acc = dot_nt(r.DM[0], weight_rows(r, l, 0, 0, n, slice(0, 3 * HALF)))
        acc += dot_nt(r.DM[1], weight_rows(r, l, 0, 1, n, slice(0, 3 * HALF)))
        r.AW[:, cols] = acc.astype(BF16)
    r.GY[...] = dot(to_grid(r, l), r.AW[...])
    gain, shift, _ = norm_back(r, l, r.GY, r.N1, r.R1, r.ln1_gain, r.S, r.S, r.YB)
    r.SG[l, 1:2, :D] = gain
    r.SG[l, 1:2, D : 2 * D] = shift


INPUTS = (
    "x", "cot", "valid", "idx_col", "idx_row", "reg_col", "reg_row", "bias",
    "ln1_gain", "ln1_bias", "qv_bias", "proj_bias", "ln2_gain", "ln2_bias", "fc1_bias", "fc2_bias",
)
SMALL_ROWS = 8


def scratch_spec():
    return dict(
        S=pltpu.VMEM((ROWS, D), F32),
        GY=pltpu.VMEM((ROWS, D), F32),
        YB=pltpu.VMEM((ROWS, D), BF16),
        GB=pltpu.VMEM((ROWS, D), BF16),
        N1=pltpu.VMEM((LAYERS, ROWS, D), F32),
        N2=pltpu.VMEM((LAYERS, ROWS, D), F32),
        R1=pltpu.VMEM((LAYERS, ROWS, 1), F32),
        R2=pltpu.VMEM((LAYERS, ROWS, 1), F32),
        YW=pltpu.VMEM((LAYERS, WROWS, D), BF16),
        Q=pltpu.VMEM((LAYERS, WROWS, D), BF16),
        K=pltpu.VMEM((LAYERS, WROWS, D), BF16),
        V=pltpu.VMEM((LAYERS, WROWS, D), BF16),
        PR=pltpu.VMEM((LAYERS, OWN * 16, PADC, 4 * PADC), BF16),
        AW=pltpu.VMEM((WROWS, D), BF16),
        AT=pltpu.VMEM((LAYERS, ROWS, D), BF16),
        Y2=pltpu.VMEM((LAYERS, ROWS, D), BF16),
        AC=pltpu.VMEM((LAYERS, ROWS, FF), BF16),
        SL=pltpu.VMEM((LAYERS, ROWS, FF), BF16),
        PB=pltpu.VMEM((ROWS, FF), BF16),
        DM=pltpu.VMEM((2, WROWS, 3 * HALF), BF16),
        TA=pltpu.VMEM((D, ROWS), BF16),
        TB=pltpu.VMEM((D, ROWS), BF16),
        TW=pltpu.VMEM((D, WROWS), BF16),
    )


def compute_kernel(names, *refs):
    r = types.SimpleNamespace(**dict(zip(names, refs)))
    r.S[...] = r.x[...].astype(F32)
    lax.fori_loop(0, LAYERS, lambda l, c: (forward(r, l), c)[1], 0)
    r.result[...] = (r.S[...] * r.valid[...]).astype(BF16)
    r.S[...] = r.cot[...].astype(F32) * r.valid[...]

    def back(i, c):
        l = LAYERS - 1 - i
        backward_mlp(r, l)
        backward_attention(r, l)
        return c

    lax.fori_loop(0, LAYERS, back, 0)
    r.gimg[...] = r.YB[...]


def compute_call(ins, w):
    z, rb = w.shape[3], w.shape[4]
    outs = dict(
        G=jax.ShapeDtypeStruct((LAYERS, 3, 2, z, rb, 1024), BF16),
        SG=jax.ShapeDtypeStruct((LAYERS, SMALL_ROWS, FF), F32),
        DS=jax.ShapeDtypeStruct((LAYERS, 4, PADC, 4 * PADC), F32),
        result=jax.ShapeDtypeStruct((ROWS, D), BF16),
        gimg=jax.ShapeDtypeStruct((ROWS, D), BF16),
    )
    scratch = scratch_spec()
    names = INPUTS + ("W",) + tuple(outs) + tuple(scratch)
    got = pl.pallas_call(
        functools.partial(compute_kernel, names),
        out_shape=list(outs.values()),
        in_specs=[pl.BlockSpec(memory_space=pltpu.VMEM)] * (len(INPUTS) + 1),
        out_specs=[pl.BlockSpec(memory_space=pltpu.VMEM)] * len(outs),
        scratch_shapes=list(scratch.values()),
        compiler_params=pltpu.CompilerParams(vmem_limit_bytes=67043328),
        name="step",
    )(*[ins[name] for name in INPUTS], w)
    return dict(zip(outs, got))


def small_inputs(images, cot, load, mp, smalls):
    idx, reg = token_maps()
    keep = OWN * TOK_IMG

    def own(arr):
        rows = lax.dynamic_slice_in_dim(arr.reshape(-1, D), mp * keep, keep, 0)
        return jnp.pad(rows, ((0, ROWS - keep), (0, 0)))

    slot = mp * OWN + jnp.arange(ROWS, dtype=jnp.int32) // TOK_IMG
    live = (slot < load) & (jnp.arange(ROWS) < keep)
    ln1_gain, ln1_bias, qv_bias, rel_table, proj_bias, ln2_gain, ln2_bias, fc1_bias, fc2_bias = smalls
    heads = rel_table.shape[1]
    entries = rel_table.shape[2]
    entry = jnp.asarray(bias_onehot().reshape(-1))
    onehot = (entry[:, None] == jnp.arange(entries, dtype=jnp.int32)[None, :]).astype(F32)
    flat = lax.dot_general(
        onehot, rel_table.reshape(LAYERS * heads, entries), (((1,), (1,)), ((), ())),
        precision=lax.Precision.HIGHEST,
    )
    bias = flat.reshape(PADC, PADC, LAYERS, heads // 4, 4).transpose(2, 3, 0, 4, 1)
    pad_key = jnp.arange(PADC)[:, None, None] >= CELLS
    bias = jnp.where(pad_key, MASKED, bias).reshape(LAYERS, heads // 4, PADC, 4 * PADC)
    row = lambda a: a.reshape(LAYERS, 1, -1)
    return dict(
        x=own(images), cot=own(cot), valid=live.astype(F32)[:, None],
        idx_col=jnp.asarray(idx)[:, :, None], idx_row=jnp.asarray(idx)[:, None, :],
        reg_col=jnp.asarray(reg)[:, :, :, None],
        reg_row=jnp.asarray(np.tile(reg, (1, 1, 4)))[:, :, None, :],
        bias=bias, ln1_gain=row(ln1_gain), ln1_bias=row(ln1_bias), qv_bias=qv_bias,
        proj_bias=row(proj_bias), ln2_gain=row(ln2_gain), ln2_bias=row(ln2_bias),
        fc1_bias=row(fc1_bias), fc2_bias=row(fc2_bias),
    )


def table_grads(ds):
    heads = 16
    entries = (2 * WIN - 1) ** 2
    entry = jnp.asarray(bias_onehot().reshape(-1))
    onehot = (entry[:, None] == jnp.arange(entries, dtype=jnp.int32)[None, :]).astype(F32)
    flat = ds.reshape(LAYERS, heads // 4, PADC, 4, PADC).transpose(0, 1, 3, 2, 4)
    return lax.dot_general(
        flat.reshape(LAYERS * heads, PADC * PADC), onehot, (((1,), (0,)), ((), ())),
        precision=lax.Precision.HIGHEST,
    ).reshape(LAYERS, heads, entries)


def pack_weights(w_qkv, w_proj, w_fc1, w_fc2):
    rows = w_qkv.shape[1]
    first = jnp.concatenate([w_qkv.reshape(LAYERS, rows, -1), w_proj.swapaxes(1, 2)], 2)
    return jnp.stack([first, w_fc1, w_fc2.swapaxes(1, 2)], 1)


def gather_plain(shard):
    full = lax.all_gather(shard, "dp", axis=2, tiled=True)
    return lax.all_gather(full, "mp", axis=2, tiled=False)


def scatter_plain(grad):
    half = lax.psum_scatter(grad, "mp", scatter_dimension=2, tiled=False)
    return lax.psum_scatter(half, "dp", scatter_dimension=2, tiled=True).astype(F32)


def per_device(
    images, loads, cotangent, ln1_gain, ln1_bias, w_qkv, qv_bias, rel_table, w_proj, proj_bias,
    ln2_gain, ln2_bias, w_fc1, fc1_bias, w_fc2, fc2_bias,
):
    mp = lax.axis_index("mp")
    n_dp = lax.axis_size("dp")
    zs = n_dp // 4
    qv_all = lax.all_gather(qv_bias, "mp", axis=2, tiled=True)
    table_all = lax.all_gather(rel_table, "mp", axis=1, tiled=True)
    fc1_all = lax.all_gather(fc1_bias, "mp", axis=1, tiled=True)
    smalls = (ln1_gain, ln1_bias, qv_all, table_all, proj_bias, ln2_gain, ln2_bias, fc1_all, fc2_bias)
    ins = small_inputs(images, cotangent, loads[0], mp, smalls)
    shard = pack_weights(w_qkv, w_proj, w_fc1, w_fc2)
    full = gather_plain(shard)
    outs = compute_call(ins, full.reshape(LAYERS, 3, 2, zs, D // zs, 1024))
    grad = scatter_plain(outs["G"].reshape(LAYERS, 3, 2, D, 1024))
    sg, tab = lax.psum((outs["SG"], table_grads(outs["DS"])), ("dp", "mp"))
    both = lax.all_gather(
        jnp.stack([outs["result"], outs["gimg"]])[:, : OWN * TOK_IMG], "mp", axis=1, tiled=True
    )
    result, gimg = both.reshape(2, 2 * OWN, TOK_IMG, D)
    rows = w_qkv.shape[1]
    q_sum = lax.dynamic_slice_in_dim(sg[:, 2, 2 * D :].reshape(LAYERS, 2, 2, HALF), mp, 1, 2)
    return (
        result,
        gimg,
        sg[:, 1, :D],
        sg[:, 1, D : 2 * D],
        grad[:, 0, :, : 3 * HALF].reshape(LAYERS, rows, 3, HALF),
        q_sum.reshape(LAYERS, 2, HALF),
        lax.dynamic_slice_in_dim(tab, mp * 8, 8, 1),
        grad[:, 0, :, 3 * HALF :].swapaxes(1, 2),
        sg[:, 2, :D],
        sg[:, 1, 2 * D : 3 * D],
        sg[:, 1, 3 * D :],
        grad[:, 1],
        lax.dynamic_slice_in_dim(sg[:, 0], mp * 1024, 1024, 1),
        grad[:, 2].swapaxes(1, 2),
        sg[:, 2, D : 2 * D],
    )


def solution(mesh):
    wq, cols = P(None, "dp", None, "mp"), P(None, "mp")
    rows_dp, cols_dp = P(None, "dp", "mp"), P(None, "mp", "dp")
    img = P("dp", None, None)
    qv, tab = P(None, None, "mp"), P(None, "mp", None)
    return jax.shard_map(
        per_device,
        mesh=mesh,
        in_specs=(
            img, P("dp"), img, P(), P(), wq, qv, tab, cols_dp, P(), P(), P(), rows_dp, cols, cols_dp, P(),
        ),
        out_specs=(img, img, P(), P(), wq, qv, tab, cols_dp, P(), P(), P(), rows_dp, cols, cols_dp, P()),
        check_vma=False,
    )
```

time: 1130 us -> 731 us (0.65)
  local copies, waits for them, and re-layouts: 266 us -> 47.9 us
  matrix products: 134 us -> 5.34 us
  other arithmetic: 129 us -> 5.28 us
  Pallas kernels: 0 us -> 77.6 us
  waiting for transfers between devices: 485 us -> 526 us
  blocking collectives: 88.3 us -> 53.2 us
    psum x13 -> x1, waiting for transfers between devices: 220 us -> 87.6 us  [per_device(): sg, tab = lax.psum((outs['SG'], table_grads(outs['DS'])), ('dp', 'mp'))]
    dot_general x78 -> x2, matrix products: 134 us -> 5.34 us  [the longest x1 3.79 us: small_inputs(): lax.dot_general(onehot, rel_table.reshape(LAYERS * heads, entries), (((1,...]
    all_gather x3, waiting for transfers between devices: 87.9 us -> 211 us  [the longest x1 125 us: gather_plain(): return lax.all_gather(full, 'mp', axis=2, tiled=False)]
    reduce_scatter x2, waiting for transfers between devices: 143 us -> 227 us  [the longest x1 143 us: scatter_plain(): half = lax.psum_scatter(grad, 'mp', scatter_dimension=2, tiled=False)]
    pallas_call x0 -> x1, Pallas kernels: none -> 77.6 us  [compute_call(): pl.pallas_call(functools.partial(compute_kernel, names), out_shape=list(o...]
    reduce_sum x51 -> x0, other arithmetic: 69.5 us -> none  [the longest x8 16.3 us: normalize_back(): gain_grad = jnp.sum(grad_y * normed, 0)]
    another operation x32 -> x5, local copies, waits for them, and re-layouts: 53.2 us -> 1.91 us  [the longest x3 1.78 us: per_device(): result, gimg = both.reshape(2, 2 * OWN, TOK_IMG, D)]
    transpose x34 -> x3, local copies, waits for them, and re-layouts: 47.3 us -> 1.59 us  [the longest x1 0.83 us: per_device(): grad[:, 2].swapaxes(1, 2)]
  transfers between devices with their start and end apart: 19 -> 6, of which waited for: 18 -> 6; matrix products, arithmetic and copies ran while one was open for 16% -> 4% of each run, Pallas kernels for 0% -> 0%
where the time goes in v1:
time: 731 us; the launch traced here: 730 us
  waiting for transfers between devices  526 us (72%)
  Pallas kernels  77.6 us (11%)
  blocking collectives  53.2 us (7%)
  local copies, waits for them, and re-layouts  47.9 us (7%)
  between operations  15.1 us (2%)
    reduce_scatter x1, waiting for transfers between devices, scatter_plain(): half = lax.psum_scatter(grad, 'mp', scatter_dimension=2, tiled=False)  143 us
    all_gather x1, waiting for transfers between devices, gather_plain(): return lax.all_gather(full, 'mp', axis=2, tiled=False)  125 us
    psum x1, waiting for transfers between devices, per_device(): sg, tab = lax.psum((outs['SG'], table_grads(outs['DS'])), ('dp', 'mp'))  87.6 us
    reduce_scatter x1, waiting for transfers between devices, scatter_plain(): lax.psum_scatter(half, 'dp', scatter_dimension=2, tiled=True).astype(F32)  84.5 us
    pallas_call x1, Pallas kernels, compute_call(): pl.pallas_call(functools.partial(compute_kernel, names), out_shape=list(o...  77.6 us
    all_gather x1, waiting for transfers between devices, gather_plain(): full = lax.all_gather(shard, 'dp', axis=2, tiled=True)  64.3 us
    psum x1, blocking collectives, per_device(): sg, tab = lax.psum((outs['SG'], table_grads(outs['DS'])), ('dp', 'mp'))  39.7 us
    all_gather x1, waiting for transfers between devices, per_device(): lax.all_gather(jnp.stack([outs['result'], outs['gimg']])[:, :OWN * TOK_IM...  21.1 us
  transfers between devices with their start and end apart: 6, of which 6 were waited for; matrix products, arithmetic and copies ran while one was open for 4% of the time, Pallas kernels for 0%

profile of v1, /device:TPU:0, one launch (start us, length us, event | category | flops | bytes accessed | tf_op | source)
XLA Modules:
  0.0 730.3 jit_solution(9489654544780282750)
XLA Ops:
  7.2 1.0 copy.76
  8.2 0.8 maximum_bitcast_fusion
  9.0 1.8 pad_maximum_fusion.1
  10.8 64.3 %all-gather.5.cloned.1.call-done = bf16[2,3,512,1024]{3,2,0,1:T(8,128)(2,1)} async-done(((bf16[2,3,32,1024]{3,2,0,1:T(8,128)(2,1)}), bf16[2,3,512,1024]{3,2,0,1:T(8,128)(2,1)}) %all-gather.5.cloned.1.call-update) | async-done | bytes 6291472 | tf_op jit(solution)/shard_map/all_gather | solution.py:446
  75.5 0.7 copy-done.1
  76.7 0.8 pad.7.refs_0_
  77.5 0.8 pad.8.refs_1_
  78.9 4.4 all_gather.21
  83.4 3.8 fusion.11
  87.1 0.7 reshape.192
  87.8 1.0 copy.67.refs_7_
  88.8 4.4 all_gather.23
  93.1 0.6 reshape.179.refs_14_
  93.7 0.6 reshape.174.refs_8_
  94.3 0.6 reshape.175.refs_9_
  94.9 0.6 reshape.176.refs_11_
  95.5 0.6 reshape.177.refs_12_
  96.1 0.6 reshape.178.refs_13_
  96.7 0.6 reshape.180.refs_15_
  97.3 4.8 all_gather.22.refs_10_
  102.1 0.7 fusion.19.refs_2_
  102.9 125.1 %all-gather.9.cloned.1.call-done = bf16[2,3,1024,1024]{3,2,0,1:T(8,128)(2,1)} async-done(((bf16[2,3,512,1024]{3,2,0,1:T(8,128)(2,1)}), bf16[2,3,1024,1024]{3,2,0,1:T(8,128)(2,1)}) %all-gather.9.cloned.1.call-update) | async-done | bytes 12582928 | tf_op jit(solution)/shard_map/all_gather | solution.py:447
  228.0 10.5 %copy.60 = bf16[2,3,1024,1024]{3,2,1,0:T(8,128)(2,1)} copy(bf16[2,3,1024,1024]{3,2,0,1:T(8,128)(2,1)} %all-gather.9.cloned.1.call-done) | data formatting | bytes 25165824 | tf_op jit(solution)/shard_map/all_gather | solution.py:447
  238.5 77.6 %step.1 = (bf16[2,3,2,4,128,1024]{5,4,3,2,1,0:T(8,128)(2,1)}, f32[2,8,2048]{2,1,0:T(8,128)}, f32[2,4,64,256]{3,2,1,0:T(8,128)}, bf16[400,512]{1,0:T(8,128)(2,1)}, bf16[400,512]{1,0:T(8,128)(2,1)}) custom-call(bf16[400,512]{1,0:T(8,128)(2,1)} %pad.7.refs_0_, bf16[400,512]{1,0:T(8,128)(2,1)} %pad.8.refs_1_, f32[400,1]{1,0:T(8,128)} %fusion.19.refs_2_, ...), custom_call_target="tpu_custom_call" | custom-call | tf_op jit(solution)/shard_map/step/pallas_call | solution.py:381
  316.1 10.5 %copy.61 = bf16[2,3,2,512,1024]{4,3,0,1,2:T(8,128)(2,1)} copy(bf16[2,3,2,512,1024]{4,3,2,1,0:T(8,128)(2,1)} %bitcast.80) | data formatting | bytes 25165824 | tf_op jit(solution)/shard_map/reshape | solution.py:470
  327.8 0.9 pad_maximum_fusion
  328.8 142.5 %reduce-scatter.3.cloned.1.call-done = bf16[2,3,1,512,1024]{4,3,0,1,2:T(8,128)(2,1)} async-done(((bf16[2,3,2,512,1024]{4,3,0,1,2:T(8,128)(2,1)}), bf16[2,3,1,512,1024]{4,3,0,1,2:T(8,128)(2,1)}) %reduce-scatter.3.cloned.1.call-update) | async-done | bytes 6291472 | tf_op jit(solution)/shard_map/reduce_scatter | solution.py:451
  472.3 1.6 fusion.4
  473.9 39.7 %psum.15 = f32[2,16,169]{2,1,0:T(8,128)S(1)} all-reduce(f32[2,16,169]{2,1,0:T(8,128)S(1)} %fusion.4), channel_id=1, replica_groups=mesh['dp'=16,'mp'=2] {'dp','mp'}, use_global_device_ids=true, to_apply=%region_3.4 | all-reduce | flops 5408 | bytes 43264 | tf_op jit(solution)/shard_map/psum | solution.py:471
  513.6 0.6 constant_dynamic-slice_fusion.1
  514.2 87.6 %all-reduce.4.cloned.1.call-done = f32[2,8,2048]{2,1,0:T(8,128)} async-done(((f32[2,8,2048]{2,1,0:T(8,128)}), f32[2,8,2048]{2,1,0:T(8,128)}) %all-reduce.4.cloned.1.call-update) | async-done | bytes 131088 | tf_op jit(solution)/shard_map/psum | solution.py:471
  601.8 0.9 slice.63
  602.7 0.6 copy.85
  603.3 0.9 slice_reduce_fusion
  604.2 0.6 copy.90
  604.8 0.9 fusion.22
  605.7 0.6 copy.86
  606.3 0.6 copy.87
  609.3 21.1 %all-gather.7.cloned.1.call-done = bf16[2,784,512]{2,1,0:T(8,128)(2,1)} async-done(((bf16[2,392,512]{2,1,0:T(8,128)(2,1)}), bf16[2,784,512]{2,1,0:T(8,128)(2,1)}) %all-gather.7.cloned.1.call-update) | async-done | bytes 1605648 | tf_op jit(solution)/shard_map/all_gather | solution.py:472
  630.4 1.5 fusion.21
  632.0 1.3 copy.63
  633.5 1.3 copy.64
  634.7 84.5 %reduce-scatter.5.cloned.1.call-done = bf16[2,3,32,1024]{3,2,0,1:T(8,128)(2,1)} async-done(((bf16[2,3,512,1024]{3,2,0,1:T(8,128)(2,1)}), bf16[2,3,32,1024]{3,2,0,1:T(8,128)(2,1)}) %reduce-scatter.5.cloned.1.call-update) | async-done | bytes 393232 | tf_op jit(solution)/shard_map/reduce_scatter | solution.py:452
  719.2 1.1 convert_element_type.19
  720.3 0.8 slice_bitcast_fusion
  721.1 0.6 slice_bitcast_fusion.2
  721.7 0.9 slice.56
  722.8 0.7 copy.65
  (63 shorter events, 5.8 us)
Async XLA Ops:
  7.2 68.0 %copy-start = (bf16[4,196,512]{2,0,1:T(4,128)(2,1)S(1)}, bf16[4,196,512]{2,0,1:T(4,128)(2,1)}, u32[]{:S(2)}) copy-start(bf16[4,196,512]{2,0,1:T(4,128)(2,1)} %param.21) | copy-start | bytes 2408452
  7.2 67.9 %all-gather.5.cloned.1.call-start = ((), (), s32[]{:S(2)}) async-start(), calls=%async_computation.2 | async-start | bytes 6684672 | tf_op jit(solution)/shard_map/all_gather | solution.py:446
  10.8 217.3 %all-gather.9.cloned.1.call-start = ((), (), s32[]{:S(2)}) async-start(), calls=%async_computation.7 | async-start | bytes 18874368 | tf_op jit(solution)/shard_map/all_gather | solution.py:447
  75.1 1.1 copy-start.1
  75.1 396.2 %reduce-scatter.3.cloned.1.call-start = ((), (), s32[]{:S(2)}) async-start(), calls=%async_computation.5 | async-start | bytes 18874368 | tf_op jit(solution)/shard_map/reduce_scatter | solution.py:451
  75.3 3.6 copy-start.5
  75.3 8.0 %copy-start.14 = (s32[64,64]{1,0:T(8,128)S(1)}, s32[64,64]{1,0:T(8,128)}, u32[]{:S(2)}) copy-start(s32[64,64]{1,0:T(8,128)} %constant.61) | copy-start | bytes 49156
  76.5 12.3 %copy-start.6 = (f32[2,1024]{1,0:T(2,128)S(1)}, f32[2,1024]{1,0:T(2,128)}, u32[]{:S(2)}) copy-start(f32[2,1024]{1,0:T(2,128)} %param.34) | copy-start | bytes 24580
  76.5 17.2 %copy-start.8 = (f32[2,512]{1,0:T(2,128)S(1)}, f32[2,512]{1,0:T(2,128)}, u32[]{:S(2)}) copy-start(f32[2,512]{1,0:T(2,128)} %param.24) | copy-start | bytes 12292
  76.5 17.8 %copy-start.9 = (f32[2,512]{1,0:T(2,128)S(1)}, f32[2,512]{1,0:T(2,128)}, u32[]{:S(2)}) copy-start(f32[2,512]{1,0:T(2,128)} %param.25) | copy-start | bytes 12292
  76.6 18.4 %copy-start.10 = (f32[2,512]{1,0:T(2,128)S(1)}, f32[2,512]{1,0:T(2,128)}, u32[]{:S(2)}) copy-start(f32[2,512]{1,0:T(2,128)} %param.30) | copy-start | bytes 12292
  76.6 19.0 %copy-start.11 = (f32[2,512]{1,0:T(2,128)S(1)}, f32[2,512]{1,0:T(2,128)}, u32[]{:S(2)}) copy-start(f32[2,512]{1,0:T(2,128)} %param.31) | copy-start | bytes 12292
  76.6 19.6 %copy-start.12 = (f32[2,512]{1,0:T(2,128)S(1)}, f32[2,512]{1,0:T(2,128)}, u32[]{:S(2)}) copy-start(f32[2,512]{1,0:T(2,128)} %param.32) | copy-start | bytes 12292
  76.6 20.1 %copy-start.13 = (f32[2,512]{1,0:T(2,128)S(1)}, f32[2,512]{1,0:T(2,128)}, u32[]{:S(2)}) copy-start(f32[2,512]{1,0:T(2,128)} %param.36) | copy-start | bytes 12292
  76.6 20.7 %copy-start.7 = (f32[2,2,256]{2,1,0:T(2,128)S(1)}, f32[2,2,256]{2,1,0:T(2,128)}, u32[]{:S(2)}) copy-start(f32[2,2,256]{2,1,0:T(2,128)} %param.27) | copy-start | bytes 12292
  326.7 1.0 copy-start.3
  326.7 1.1 copy-start.4
  326.7 275.1 %all-reduce.4.cloned.1.call-start = ((), (), s32[]{:S(2)}) async-start(), calls=%async_computation.4 | async-start | bytes 262144 | tf_op jit(solution)/shard_map/psum | solution.py:471
  327.3 303.1 %all-gather.7.cloned.1.call-start = ((), (), s32[]{:S(2)}) async-start(), calls=%async_computation.3 | async-start | bytes 2408448 | tf_op jit(solution)/shard_map/all_gather | solution.py:472
  327.8 143.6 %copy-start.2 = (f32[2,4,64,256]{3,2,1,0:T(8,128)S(1)}, f32[2,4,64,256]{3,2,1,0:T(8,128)}, u32[]{:S(2)}) copy-start(f32[2,4,64,256]{3,2,1,0:T(8,128)} %get-tuple-element.24) | copy-start | bytes 1572868
  328.8 390.5 %reduce-scatter.5.cloned.1.call-start = ((), (), s32[]{:S(2)}) async-start(), calls=%async_computation.6 | async-start | bytes 6684672 | tf_op jit(solution)/shard_map/reduce_scatter | solution.py:452
  471.3 1.0 copy-start.15
Sparse Core Ops, SparseCore 0:
  10.9 64.1 all-gather.4
  76.6 151.3 all-gather.8
  326.8 144.4 reduce-scatter.2
  477.3 124.4 all-reduce.3
  603.7 26.5 all-gather.6
  634.1 85.0 reduce-scatter.4

commit v2 on v1

--- a/solution.py
+++ b/solution.py
@@ -101,19 +101,19 @@
 
 
 def weight(r, l, g, x, cols):
-    part = r.W[l, g, x, :, :, cols]
+    part = r.W[l, g, x, :, :, :, :, cols]
     return part.reshape(D, part.shape[-1])
 
 
 def weight_rows(r, l, g, x, n, cols):
-    per = HALF // r.W.shape[4]
-    part = r.W[l, g, x, pl.ds(n * per, per), :, cols]
+    per = r.W.shape[3] // 2
+    part = r.W[l, g, x, pl.ds(n * per, per), :, :, :, cols]
     return part.reshape(HALF, part.shape[-1])
 
 
 def put_grad(r, l, g, x, cols, value):
-    z, rb = r.G.shape[3], r.G.shape[4]
-    r.G[l, g, x, :, :, cols] = value.astype(BF16).reshape(z, rb, value.shape[-1])
+    lead = r.G.shape[3:7]
+    r.G[l, g, x, :, :, :, :, cols] = value.astype(BF16).reshape(lead + value.shape[-1:])
 
 
 def norm_into(r, l, src, normed, rstd_ref, gain, shift, out):
@@ -368,9 +368,8 @@
 
 
 def compute_call(ins, w):
-    z, rb = w.shape[3], w.shape[4]
     outs = dict(
-        G=jax.ShapeDtypeStruct((LAYERS, 3, 2, z, rb, 1024), BF16),
+        G=jax.ShapeDtypeStruct(w.shape, BF16),
         SG=jax.ShapeDtypeStruct((LAYERS, SMALL_ROWS, FF), F32),
         DS=jax.ShapeDtypeStruct((LAYERS, 4, PADC, 4 * PADC), F32),
         result=jax.ShapeDtypeStruct((ROWS, D), BF16),
@@ -442,6 +441,334 @@
     return jnp.stack([first, w_fc1, w_fc2.swapaxes(1, 2)], 1)
 
 
+MESH = pl.DeviceIdType.MESH
+UNITS = 3 * LAYERS
+Z_SIDE = 4
+
+
+class Place:
+    def __init__(self):
+        self.dp = lax.axis_index("dp")
+        self.x = lax.axis_index("mp")
+        self.c = lax.rem(self.dp, 2)
+        self.y = lax.rem(self.dp // 2, 2)
+        self.z = self.dp // 4
+        self.sib = {"dp": self.dp + 1 - 2 * self.c, "mp": self.x}
+        self.ynbr = {"dp": self.dp + 2 - 4 * self.y, "mp": self.x}
+        self.xnbr = {"dp": self.dp, "mp": 1 - self.x}
+
+    def zpos(self, k):
+        return lax.rem(self.z + k, Z_SIDE)
+
+    def zpeer(self, k):
+        return {"dp": self.zpos(k) * 4 + lax.rem(self.dp, 4), "mp": self.x}
+
+    def peers(self):
+        return [self.sib, self.ynbr, self.xnbr] + [self.zpeer(k) for k in range(1, Z_SIDE)]
+
+
+def greet(place):
+    barrier = pltpu.get_barrier_semaphore()
+    peers = place.peers()
+    for peer in peers:
+        pl.semaphore_signal(barrier, inc=1, device_id=peer, device_id_type=MESH)
+    pl.semaphore_wait(barrier, len(peers))
+
+
+def remote(src, dst, sems, u, k, peer):
+    return pltpu.make_async_remote_copy(
+        src_ref=src, dst_ref=dst, send_sem=sems.at[0, u, k], recv_sem=sems.at[1, u, k],
+        device_id=peer, device_id_type=MESH,
+    )
+
+
+def landed(dst, sems, u, k, peer):
+    remote(dst, dst, sems, u, k, peer).wait_recv()
+
+
+TOP, LOW = pl.ds(0, 16), pl.ds(16, 16)
+
+
+class Gather:
+    def __init__(self, place, shard, w, sems, local):
+        self.p, self.shard, self.w, self.sems, self.local = place, shard, w, sems, local
+
+    def slab(self, u, x, y, c, part=None):
+        ref = self.w.at[u // 3, lax.rem(u, 3), x, :, y, c]
+        return ref if part is None else ref.at[:, part]
+
+    def block(self, u, z):
+        p = self.p
+        return self.w.at[u // 3, lax.rem(u, 3), p.x, z, p.y, p.c]
+
+    def own(self, u):
+        return self.shard.at[u // 3, lax.rem(u, 3)]
+
+    def z_copy(self, u, k):
+        return remote(self.own(u), self.block(u, self.p.z), self.sems, u, k - 1, self.p.zpeer(k))
+
+    def local_copy(self, u):
+        return pltpu.make_async_copy(self.own(u), self.block(u, self.p.z), self.local.at[u])
+
+    def full_copies(self, u):
+        p = self.p
+        mine = self.slab(u, p.x, p.y, p.c)
+        return [
+            remote(mine, mine, self.sems, u, 3, p.xnbr),
+            remote(mine, mine, self.sems, u, 4, p.ynbr),
+            remote(mine, mine, self.sems, u, 5, p.sib),
+        ]
+
+    def half_copies(self, u):
+        p = self.p
+        from_y, from_x = (p.x, 1 - p.y, p.c), (1 - p.x, p.y, p.c)
+        top, low = self.slab(u, *from_y, TOP), self.slab(u, *from_x, LOW)
+        fy, fx = self.slab(u, *from_y), self.slab(u, *from_x)
+        return [
+            remote(top, top, self.sems, u, 6, p.xnbr),
+            remote(low, low, self.sems, u, 7, p.ynbr),
+            remote(fx, fx, self.sems, u, 8, p.sib),
+            remote(fy, fy, self.sems, u, 9, p.sib),
+        ]
+
+    def last_copies(self, u):
+        p = self.p
+        far = self.slab(u, 1 - p.x, 1 - p.y, p.c)
+        return [remote(far, far, self.sems, u, 10, p.sib)]
+
+    def start_own(self, u):
+        self.local_copy(u).start()
+        for k in range(1, Z_SIDE):
+            self.z_copy(u, k).start()
+
+    def pass_own(self, u):
+        p = self.p
+        self.local_copy(u).wait()
+        for k in range(1, Z_SIDE):
+            landed(self.block(u, p.zpos(Z_SIDE - k)), self.sems, u, k - 1, p.zpeer(Z_SIDE - k))
+        for copy in self.full_copies(u):
+            copy.start()
+
+    def pass_near(self, u):
+        p = self.p
+        landed(self.slab(u, 1 - p.x, p.y, p.c), self.sems, u, 3, p.xnbr)
+        landed(self.slab(u, p.x, 1 - p.y, p.c), self.sems, u, 4, p.ynbr)
+        for copy in self.half_copies(u):
+            copy.start()
+
+    def pass_far(self, u):
+        p = self.p
+        landed(self.slab(u, 1 - p.x, 1 - p.y, p.c, TOP), self.sems, u, 6, p.xnbr)
+        landed(self.slab(u, 1 - p.x, 1 - p.y, p.c, LOW), self.sems, u, 7, p.ynbr)
+        for copy in self.last_copies(u):
+            copy.start()
+
+    def ready(self, u):
+        p = self.p
+        for k, (x, y) in ((5, (p.x, p.y)), (8, (1 - p.x, p.y)), (9, (p.x, 1 - p.y)), (10, (1 - p.x, 1 - p.y))):
+            landed(self.slab(u, x, y, 1 - p.c), self.sems, u, k, p.sib)
+
+    def tick(self, t):
+        @pl.when(t < UNITS)
+        def _():
+            self.pass_own(t)
+
+        @pl.when(t + 2 < UNITS)
+        def _():
+            self.start_own(t + 2)
+
+        @pl.when((t >= 1) & (t - 1 < UNITS))
+        def _():
+            self.pass_near(t - 1)
+
+        @pl.when((t >= 2) & (t - 2 < UNITS))
+        def _():
+            self.pass_far(t - 2)
+
+    def drain(self, u):
+        for k in range(1, Z_SIDE):
+            self.z_copy(u, k).wait_send()
+        for copy in self.full_copies(u) + self.half_copies(u) + self.last_copies(u):
+            copy.wait_send()
+
+
+def gather_kernel(shard, w, sems, local):
+    place = Place()
+    greet(place)
+    gather = Gather(place, shard, w, sems, local)
+    gather.start_own(0)
+    gather.start_own(1)
+
+    def tick(t, c):
+        gather.tick(t)
+        return c
+
+    lax.fori_loop(0, UNITS + 2, tick, 0)
+
+    def finish(u, c):
+        gather.ready(u)
+        gather.drain(u)
+        return c
+
+    lax.fori_loop(0, UNITS, finish, 0)
+
+
+def gather_call(shard):
+    return pl.pallas_call(
+        gather_kernel,
+        out_shape=jax.ShapeDtypeStruct((LAYERS, 3, 2, Z_SIDE, 2, 2, 32, 1024), BF16),
+        in_specs=[pl.BlockSpec(memory_space=pltpu.VMEM)],
+        out_specs=pl.BlockSpec(memory_space=pltpu.VMEM),
+        scratch_shapes=[pltpu.SemaphoreType.DMA((2, UNITS, 11)), pltpu.SemaphoreType.DMA((UNITS,))],
+        compiler_params=pltpu.CompilerParams(
+            collective_id=0, has_side_effects=True, vmem_limit_bytes=40 << 20
+        ),
+        name="gather",
+    )(shard)
+
+
+class Scatter:
+    def __init__(self, place, r):
+        self.p, self.r, self.sems = place, r, r.sums
+
+    def at(self, ref, u):
+        return ref.at[u // 3, lax.rem(u, 3)]
+
+    def sib_copy(self, u):
+        p, r = self.p, self.r
+        return remote(
+            self.at(r.G, u).at[:, :, :, 1 - p.c], self.at(r.P, u), self.sems, u, 0, p.sib
+        )
+
+    def part(self, u, x, y, rows=None):
+        ref = self.at(self.r.P, u).at[x, :, y]
+        return ref if rows is None else ref.at[:, rows]
+
+    def far_copies(self, u):
+        p, r = self.p, self.r
+        return [
+            remote(self.part(u, 1 - p.x, 1 - p.y, TOP), self.at(r.RA, u).at[0], self.sems, u, 1, p.xnbr),
+            remote(self.part(u, 1 - p.x, 1 - p.y, LOW), self.at(r.RA, u).at[1], self.sems, u, 2, p.ynbr),
+        ]
+
+    def near_copies(self, u):
+        p, r = self.p, self.r
+        return [
+            remote(self.part(u, 1 - p.x, p.y), self.at(r.RB, u).at[0], self.sems, u, 3, p.xnbr),
+            remote(self.part(u, p.x, 1 - p.y), self.at(r.RB, u).at[1], self.sems, u, 4, p.ynbr),
+        ]
+
+    def z_copy(self, u, k):
+        p, r = self.p, self.r
+        src = self.at(r.P, u).at[p.x, p.zpos(k), p.y]
+        return remote(src, self.at(r.RC, u).at[k - 1], self.sems, u, 4 + k, p.zpeer(k))
+
+    def start_sib(self, u):
+        self.sib_copy(u).start()
+
+    def add(self, dst, *srcs):
+        for z in range(Z_SIDE):
+            total = dst[z].astype(F32)
+            for src in srcs:
+                total = total + src[z].astype(F32)
+            dst[z] = total.astype(BF16)
+
+    def start_far(self, u):
+        p, r = self.p, self.r
+        landed(self.at(r.P, u), self.sems, u, 0, p.sib)
+        grads = self.at(r.G, u)
+        self.add(self.part(u, 1 - p.x, 1 - p.y), grads.at[1 - p.x, :, 1 - p.y, p.c])
+        for copy in self.far_copies(u):
+            copy.start()
+        for x, y in ((1 - p.x, p.y), (p.x, 1 - p.y), (p.x, p.y)):
+            self.add(self.part(u, x, y), grads.at[x, :, y, p.c])
+
+    def start_near(self, u):
+        p, r = self.p, self.r
+        landed(self.at(r.RA, u).at[0], self.sems, u, 1, p.xnbr)
+        landed(self.at(r.RA, u).at[1], self.sems, u, 2, p.ynbr)
+        self.add(self.part(u, p.x, 1 - p.y, TOP), self.at(r.RA, u).at[0])
+        self.add(self.part(u, 1 - p.x, p.y, LOW), self.at(r.RA, u).at[1])
+        for copy in self.near_copies(u):
+            copy.start()
+
+    def start_z(self, u):
+        p, r = self.p, self.r
+        landed(self.at(r.RB, u).at[0], self.sems, u, 3, p.xnbr)
+        landed(self.at(r.RB, u).at[1], self.sems, u, 4, p.ynbr)
+        self.add(self.part(u, p.x, p.y), self.at(r.RB, u).at[0], self.at(r.RB, u).at[1])
+        for k in range(1, Z_SIDE):
+            self.z_copy(u, k).start()
+
+    def finish(self, u):
+        p, r = self.p, self.r
+        total = r.P[u // 3, lax.rem(u, 3), p.x, p.z, p.y].astype(F32)
+        for k in range(1, Z_SIDE):
+            landed(self.at(r.RC, u).at[k - 1], self.sems, u, 4 + k, p.zpeer(Z_SIDE - k))
+            total = total + r.RC[u // 3, lax.rem(u, 3), k - 1].astype(F32)
+        r.grad[u // 3, lax.rem(u, 3)] = total
+
+    def drain(self, u):
+        for copy in [self.sib_copy(u)] + self.far_copies(u) + self.near_copies(u):
+            copy.wait_send()
+        for k in range(1, Z_SIDE):
+            self.z_copy(u, k).wait_send()
+
+
+def scatter_scratch():
+    lead = (LAYERS, 3)
+    return dict(
+        P=pltpu.VMEM(lead + (2, Z_SIDE, 2, 32, 1024), BF16),
+        RA=pltpu.VMEM(lead + (2, Z_SIDE, 16, 1024), BF16),
+        RB=pltpu.VMEM(lead + (2, Z_SIDE, 32, 1024), BF16),
+        RC=pltpu.VMEM(lead + (3, 32, 1024), BF16),
+        sums=pltpu.SemaphoreType.DMA((2, UNITS, 8)),
+    )
+
+
+def scatter_kernel(names, *refs):
+    r = types.SimpleNamespace(**dict(zip(names, refs)))
+    place = Place()
+    greet(place)
+    scatter = Scatter(place, r)
+
+    def tick(t, c):
+        for lag, stage in enumerate(
+            (scatter.start_sib, scatter.start_far, scatter.start_near, scatter.start_z, scatter.finish)
+        ):
+            u = t - lag
+
+            @pl.when((u >= 0) & (u < UNITS))
+            def _():
+                stage(u)
+
+        return c
+
+    lax.fori_loop(0, UNITS + 4, tick, 0)
+
+    def finish(u, c):
+        scatter.drain(u)
+        return c
+
+    lax.fori_loop(0, UNITS, finish, 0)
+
+
+def scatter_call(g):
+    scratch = scatter_scratch()
+    names = ("G", "grad") + tuple(scratch)
+    return pl.pallas_call(
+        functools.partial(scatter_kernel, names),
+        out_shape=jax.ShapeDtypeStruct((LAYERS, 3, 32, 1024), F32),
+        in_specs=[pl.BlockSpec(memory_space=pltpu.VMEM)],
+        out_specs=pl.BlockSpec(memory_space=pltpu.VMEM),
+        scratch_shapes=list(scratch.values()),
+        compiler_params=pltpu.CompilerParams(
+            collective_id=1, has_side_effects=True, vmem_limit_bytes=48 << 20
+        ),
+        name="scatter",
+    )(g)
+
+
 def gather_plain(shard):
     full = lax.all_gather(shard, "dp", axis=2, tiled=True)
     return lax.all_gather(full, "mp", axis=2, tiled=False)
@@ -458,16 +785,22 @@
 ):
     mp = lax.axis_index("mp")
     n_dp = lax.axis_size("dp")
-    zs = n_dp // 4
     qv_all = lax.all_gather(qv_bias, "mp", axis=2, tiled=True)
     table_all = lax.all_gather(rel_table, "mp", axis=1, tiled=True)
     fc1_all = lax.all_gather(fc1_bias, "mp", axis=1, tiled=True)
     smalls = (ln1_gain, ln1_bias, qv_all, table_all, proj_bias, ln2_gain, ln2_bias, fc1_all, fc2_bias)
     ins = small_inputs(images, cotangent, loads[0], mp, smalls)
     shard = pack_weights(w_qkv, w_proj, w_fc1, w_fc2)
-    full = gather_plain(shard)
-    outs = compute_call(ins, full.reshape(LAYERS, 3, 2, zs, D // zs, 1024))
-    grad = scatter_plain(outs["G"].reshape(LAYERS, 3, 2, D, 1024))
+    direct = n_dp == 4 * Z_SIDE and lax.axis_size("mp") == 2
+    if direct:
+        full = gather_call(shard)
+    else:
+        full = gather_plain(shard).reshape(LAYERS, 3, 2, 4, 1, 1, D // 4, 1024)
+    outs = compute_call(ins, full)
+    if direct:
+        grad = scatter_call(outs["G"])
+    else:
+        grad = scatter_plain(outs["G"].reshape(LAYERS, 3, 2, D, 1024))
     sg, tab = lax.psum((outs["SG"], table_grads(outs["DS"])), ("dp", "mp"))
     both = lax.all_gather(
         jnp.stack([outs["result"], outs["gimg"]])[:, : OWN * TOK_IMG], "mp", axis=1, tiled=True

time: 731 us -> 364 us (0.50)
  waiting for transfers between devices: 526 us -> 22.6 us
  Pallas kernels: 77.6 us -> 233 us
  local copies, waits for them, and re-layouts: 47.9 us -> 29.5 us
    reduce_scatter x2 -> x0, waiting for transfers between devices: 227 us -> none  [the longest x1 143 us: scatter_plain(): half = lax.psum_scatter(grad, 'mp', scatter_dimension=2, tiled=False)]
    all_gather x2 -> x0, waiting for transfers between devices: 189 us -> none  [the longest x1 125 us: gather_plain(): return lax.all_gather(full, 'mp', axis=2, tiled=False)]
    pallas_call x0 -> x2, Pallas kernels: none -> 156 us  [the longest x1 88.5 us: scatter_call(): pl.pallas_call(functools.partial(scatter_kernel, names), out_shape=jax.Sh...]
    psum x1, waiting for transfers between devices: 87.6 us -> 22.6 us  [per_device(): sg, tab = lax.psum((outs['SG'], table_grads(outs['DS'])), ('dp', 'mp'))]
    all_gather x1, waiting for transfers between devices: 21.1 us -> 0.01 us  [per_device(): lax.all_gather(jnp.stack([outs['result'], outs['gimg']])[:, :OWN * TOK_IM...]
    reshape x1 -> x0, local copies, waits for them, and re-layouts: 10.5 us -> none  [per_device(): grad = scatter_plain(outs['G'].reshape(LAYERS, 3, 2, D, 1024))]
    all_gather x1 -> x0, local copies, waits for them, and re-layouts: 10.5 us -> none  [gather_plain(): return lax.all_gather(full, 'mp', axis=2, tiled=False)]
  transfers between devices with their start and end apart: 6 -> 2, of which waited for: 6 -> 1; matrix products, arithmetic and copies ran while one was open for 4% -> 4% of each run, Pallas kernels for 0% -> 24%
where the time goes in v2:
time: 364 us
  Pallas kernels  233 us (64%)
  blocking collectives  53.2 us (15%)
  local copies, waits for them, and re-layouts  29.5 us (8%)
  waiting for transfers between devices  22.6 us (6%)
  between operations  16.5 us (5%)
  matrix products  5.34 us (1%)
    pallas_call x1, Pallas kernels, scatter_call(): pl.pallas_call(functools.partial(scatter_kernel, names), out_shape=jax.Sh...  88.5 us
    pallas_call x1, Pallas kernels, compute_call(): pl.pallas_call(functools.partial(compute_kernel, names), out_shape=list(o...  77.6 us
    pallas_call x1, Pallas kernels, gather_call(): pl.pallas_call(gather_kernel, out_shape=jax.ShapeDtypeStruct((LAYERS, 3,...  67.1 us
    psum x1, blocking collectives, per_device(): sg, tab = lax.psum((outs['SG'], table_grads(outs['DS'])), ('dp', 'mp'))  39.8 us
    psum x1, waiting for transfers between devices, per_device(): sg, tab = lax.psum((outs['SG'], table_grads(outs['DS'])), ('dp', 'mp'))  22.6 us
    unnamed x49, local copies, waits for them, and re-layouts  14.1 us
  transfers between devices with their start and end apart: 2, of which 1 were waited for; matrix products, arithmetic and copies ran while one was open for 4% of the time, Pallas kernels for 24%

profile of v2, /device:TPU:0, one launch (start us, length us, event | category | flops | bytes accessed | tf_op | source)
XLA Modules:
  0.0 363.6 jit_solution(17426345050397211274)
XLA Ops:
  8.1 1.3 copy.52
  9.4 0.1 reshape.165
  9.8 0.1 reshape.166
  10.0 0.8 pad.7.refs_0_
  10.8 0.8 pad.8.refs_1_
  12.4 67.1 %gather.1.refs_16_ = bf16[2,3,2,4,2,2,32,1024]{7,6,5,4,3,2,1,0:T(8,128)(2,1)S(1)} custom-call(bf16[2,3,32,1024]{3,2,1,0:T(8,128)(2,1)S(1)} %pad_maximum_fusion.1.shard), custom_call_target="tpu_custom_call" | custom-call | tf_op jit(solution)/shard_map/gather/pallas_call | solution.py:617
  79.5 4.5 %copy-done = bf16[2,3,2,4,2,2,32,1024]{7,6,5,4,3,2,1,0:T(8,128)(2,1)} copy-done((bf16[2,3,2,4,2,2,32,1024]{7,6,5,4,3,2,1,0:T(8,128)(2,1)}, bf16[2,3,2,4,2,2,32,1024]{7,6,5,4,3,2,1,0:T(8,128)(2,1)S(1)}, u32[]{:S(2)}) %copy-start) | copy-done | bytes 12582936
  84.1 4.5 %all_gather.12 = f32[2,16,169]{2,1,0:T(8,128)S(1)} all-gather(f32[2,8,169]{2,1,0:T(8,128)S(1)} %copy-done.7), channel_id=1, replica_groups=mesh['dp'=16,'mp'=2] {'mp'}, dimensions={1}, use_global_device_ids=true | all-gather | bytes 32448 | tf_op jit(solution)/shard_map/all_gather | solution.py:789
  88.7 3.8 %fusion.11 = f32[2,4,64,4,64]{4,3,1,0,2:T(4,128)S(1)} fusion(f32[2,4,4,169,1]{3,2,1,0,4:T(4,128)S(1)} %reshape.179, s32[64,64]{1,0:T(8,128)S(1)} %copy-done.16, pred[64]{0:T(512)(128)(4,1)S(1)} %iota_compare_fusion.3), kind=kOutput, calls=%fused_computation.9 | convolution fusion | flops 266637312 | bytes 562368 | tf_op jit(solution)/shard_map/dot_general | solution.py:407
  92.5 0.7 reshape.182
  93.1 1.0 copy.62.refs_7_
  94.1 4.3 %all_gather.14 = f32[2,2048]{1,0:T(2,128)S(1)} all-gather(f32[2,1024]{1,0:T(2,128)S(1)} %copy-done.8), channel_id=1, replica_groups=mesh['dp'=16,'mp'=2] {'mp'}, dimensions={1}, use_global_device_ids=true | all-gather | bytes 24576 | tf_op jit(solution)/shard_map/all_gather | solution.py:790
  98.4 0.6 reshape.173.refs_14_
  99.1 4.5 %all_gather.13.refs_10_ = f32[2,2,512]{2,1,0:T(2,128)} all-gather(f32[2,2,256]{2,1,0:T(2,128)S(1)} %copy-done.9), channel_id=1, replica_groups=mesh['dp'=16,'mp'=2] {'mp'}, dimensions={2}, use_global_device_ids=true | all-gather | bytes 12288 | tf_op jit(solution)/shard_map/all_gather | solution.py:788
  103.5 0.6 reshape.168.refs_8_
  104.1 0.6 reshape.169.refs_9_
  104.7 0.6 reshape.170.refs_11_
  105.3 0.6 reshape.171.refs_12_
  105.9 0.6 reshape.172.refs_13_
  106.5 0.6 reshape.174.refs_15_
  107.1 0.7 fusion.19.refs_2_
  107.9 77.6 %step.1 = (bf16[2,3,2,4,2,2,32,1024]{7,6,5,4,3,2,1,0:T(8,128)(2,1)}, f32[2,8,2048]{2,1,0:T(8,128)}, f32[2,4,64,256]{3,2,1,0:T(8,128)}, bf16[400,512]{1,0:T(8,128)(2,1)}, bf16[400,512]{1,0:T(8,128)(2,1)}) custom-call(bf16[400,512]{1,0:T(8,128)(2,1)} %pad.7.refs_0_, bf16[400,512]{1,0:T(8,128)(2,1)} %pad.8.refs_1_, f32[400,1]{1,0:T(8,128)} %fusion.19.refs_2_, ...), custom_call_target="tpu_custom_call" | custom-call | tf_op jit(solution)/shard_map/step/pallas_call | solution.py:380
  185.5 0.3 all-gather.2.cloned.1.call-start
  185.8 2.1 pad_maximum_fusion
  187.8 0.5 reshape.177
  188.4 0.4 dot_general.12
  188.8 88.5 %scatter.1 = f32[2,3,32,1024]{3,2,1,0:T(8,128)S(1)} custom-call(bf16[2,3,2,4,2,2,32,1024]{7,6,5,4,3,2,1,0:T(8,128)(2,1)} %get-tuple-element.23.refs_0_), custom_call_target="tpu_custom_call" | custom-call | tf_op jit(solution)/shard_map/scatter/pallas_call | solution.py:759
  277.5 0.7 copy.60
  278.2 1.6 fusion.4
  279.8 39.8 %psum.15 = f32[2,16,169]{2,1,0:T(8,128)S(1)} all-reduce(f32[2,16,169]{2,1,0:T(8,128)S(1)} %fusion.4), channel_id=1, replica_groups=mesh['dp'=16,'mp'=2] {'dp','mp'}, use_global_device_ids=true, to_apply=%region_1.2 | all-reduce | flops 5408 | bytes 43264 | tf_op jit(solution)/shard_map/psum | solution.py:804
  319.6 0.6 constant_dynamic-slice_fusion.1
  320.2 0.6 slice_bitcast_fusion.2
  320.9 0.8 slice_bitcast_fusion
  321.7 22.6 %all-reduce.4.cloned.1.call-done = f32[2,8,2048]{2,1,0:T(8,128)} async-done(((f32[2,8,2048]{2,1,0:T(8,128)}), f32[2,8,2048]{2,1,0:T(8,128)}) %all-reduce.4.cloned.1.call-update) | async-done | bytes 131088 | tf_op jit(solution)/shard_map/psum | solution.py:804
  344.3 0.9 slice.60
  345.2 0.6 copy.80
  345.8 0.9 slice_reduce_fusion
  346.7 0.6 copy.85
  347.3 0.9 fusion.22
  348.2 0.6 copy.81
  348.8 0.6 copy.82
  349.4 0.6 copy.83
  350.0 0.6 copy.84
  350.6 0.6 copy.86
  351.2 0.6 copy.87
  351.8 1.5 fusion.21
  353.4 1.3 copy.58
  354.9 1.3 copy.59
  (54 shorter events, 1.1 us)
Async XLA Ops:
  8.0 1.6 copy-start.1
  8.0 336.3 %all-reduce.4.cloned.1.call-start = ((), (), s32[]{:S(2)}) async-start(), calls=%async_computation.1 | async-start | bytes 262144 | tf_op jit(solution)/shard_map/psum | solution.py:804
  9.6 2.6 copy-start.5
  9.8 2.5 copy-start.6
  9.8 2.5 copy-start.3
  9.8 2.5 copy-start.4
  12.4 71.6 %copy-start.7 = (f32[2,8,169]{2,1,0:T(8,128)S(1)}, f32[2,8,169]{2,1,0:T(8,128)}, u32[]{:S(2)}) copy-start(f32[2,8,169]{2,1,0:T(8,128)} %param.28) | copy-start | bytes 32452
  12.4 76.3 %copy-start.16 = (s32[64,64]{1,0:T(8,128)S(1)}, s32[64,64]{1,0:T(8,128)}, u32[]{:S(2)}) copy-start(s32[64,64]{1,0:T(8,128)} %constant.61) | copy-start | bytes 49156
  79.5 4.5 %copy-start = (bf16[2,3,2,4,2,2,32,1024]{7,6,5,4,3,2,1,0:T(8,128)(2,1)}, bf16[2,3,2,4,2,2,32,1024]{7,6,5,4,3,2,1,0:T(8,128)(2,1)S(1)}, u32[]{:S(2)}) copy-start(bf16[2,3,2,4,2,2,32,1024]{7,6,5,4,3,2,1,0:T(8,128)(2,1)S(1)} %gather.1.refs_16_) | copy-start | bytes 37748740
  84.0 10.1 %copy-start.8 = (f32[2,1024]{1,0:T(2,128)S(1)}, f32[2,1024]{1,0:T(2,128)}, u32[]{:S(2)}) copy-start(f32[2,1024]{1,0:T(2,128)} %param.34) | copy-start | bytes 24580
  84.0 15.0 %copy-start.9 = (f32[2,2,256]{2,1,0:T(2,128)S(1)}, f32[2,2,256]{2,1,0:T(2,128)}, u32[]{:S(2)}) copy-start(f32[2,2,256]{2,1,0:T(2,128)} %param.27) | copy-start | bytes 12292
  84.0 19.5 %copy-start.10 = (f32[2,512]{1,0:T(2,128)S(1)}, f32[2,512]{1,0:T(2,128)}, u32[]{:S(2)}) copy-start(f32[2,512]{1,0:T(2,128)} %param.24) | copy-start | bytes 12292
  84.0 20.1 %copy-start.11 = (f32[2,512]{1,0:T(2,128)S(1)}, f32[2,512]{1,0:T(2,128)}, u32[]{:S(2)}) copy-start(f32[2,512]{1,0:T(2,128)} %param.25) | copy-start | bytes 12292
  84.0 20.7 %copy-start.12 = (f32[2,512]{1,0:T(2,128)S(1)}, f32[2,512]{1,0:T(2,128)}, u32[]{:S(2)}) copy-start(f32[2,512]{1,0:T(2,128)} %param.30) | copy-start | bytes 12292
  84.1 21.3 %copy-start.13 = (f32[2,512]{1,0:T(2,128)S(1)}, f32[2,512]{1,0:T(2,128)}, u32[]{:S(2)}) copy-start(f32[2,512]{1,0:T(2,128)} %param.31) | copy-start | bytes 12292
  84.1 21.9 %copy-start.14 = (f32[2,512]{1,0:T(2,128)S(1)}, f32[2,512]{1,0:T(2,128)}, u32[]{:S(2)}) copy-start(f32[2,512]{1,0:T(2,128)} %param.32) | copy-start | bytes 12292
  84.1 22.4 %copy-start.15 = (f32[2,512]{1,0:T(2,128)S(1)}, f32[2,512]{1,0:T(2,128)}, u32[]{:S(2)}) copy-start(f32[2,512]{1,0:T(2,128)} %param.36) | copy-start | bytes 12292
  185.5 2.4 copy-start.2
  185.5 166.3 %all-gather.2.cloned.1.call-start = ((), (), s32[]{:S(2)}) async-start(), calls=%async_computation | async-start | bytes 2408448 | tf_op jit(solution)/shard_map/all_gather | solution.py:805
  188.8 89.4 %copy-start.17 = (s32[4096]{0:T(1024)S(1)}, s32[4096]{0:T(1024)}, u32[]{:S(2)}) copy-start(s32[4096]{0:T(1024)} %constant.46.clone) | copy-start | bytes 49156
Sparse Core Ops, SparseCore 0:
  185.6 158.6 all-reduce.3
Sparse Core Ops, SparseCore 1:
  188.1 47.2 all-gather.1

commit v3 on v2

v3 whole, which is shorter than its diff:
```python
import functools
import types

import jax
import jax.numpy as jnp
import numpy as np
from jax import lax
from jax.experimental import pallas as pl
from jax.experimental.pallas import tpu as pltpu
from jax.sharding import PartitionSpec as P

D = 512
HD = 32
FF = 2048
SIDE = 14
WIN = 7
SHIFT = 3
LAYERS = 2
TOK_IMG = SIDE * SIDE
CELLS = WIN * WIN
PADC = 64
EPS = 1e-05
MASKED = -1e30
INV_ROOT_TWO = 0.7071067811865476
INV_ROOT_TWOPI = 0.3989422804014327
SCALE_Q = HD**-0.5

OWN = 2
ROWS = 400
WROWS = OWN * 4 * PADC
STEP = 80
HALF = 256
F32 = jnp.float32
BF16 = jnp.bfloat16


def token_maps():
    idx = np.full((LAYERS, WROWS), -1, np.int32)
    reg = np.zeros((LAYERS, 4, PADC), np.int32)
    for layer in range(LAYERS):
        shift = SHIFT if layer % 2 else 0
        for win in range(OWN * 4):
            img, wr, wc = win // 4, (win // 2) % 2, win % 2
            for cell in range(CELLS):
                r, c = wr * WIN + cell // WIN, wc * WIN + cell % WIN
                token = ((r + shift) % SIDE) * SIDE + (c + shift) % SIDE
                idx[layer, win * PADC + cell] = token * OWN + img
                if shift:
                    band = lambda v: 0 if v < SIDE - WIN else (1 if v < SIDE - SHIFT else 2)
                    reg[layer, win % 4, cell] = 3 * band(r) + band(c)
    return idx, reg


def dot(a, b):
    return jnp.dot(a, b, preferred_element_type=F32)


def dot_nt(a, b):
    return lax.dot_general(a, b, (((1,), (1,)), ((), ())), preferred_element_type=F32)


def dot_tn(a, b):
    return lax.dot_general(a, b, (((0,), (0,)), ((), ())), preferred_element_type=F32)


def lane_head(shape):
    return lax.broadcasted_iota(jnp.int32, shape, 1) // HD


def spread_heads(block):
    head = lane_head(block.shape)
    zero = jnp.zeros_like(block)
    return jnp.concatenate([jnp.where(head == h, block, zero) for h in range(4)], axis=0)


def gather_heads(stack):
    head = lane_head((PADC, 128))
    total = jnp.where(head == 0, stack[:PADC], 0.0)
    for h in range(1, 4):
        total = total + jnp.where(head == h, stack[h * PADC : (h + 1) * PADC], 0.0)
    return total


def row_loop(body, init):
    def step(i, carry):
        return body(pl.ds(pl.multiple_of(i * STEP, STEP), STEP), carry)

    return lax.fori_loop(0, ROWS // STEP, step, init)


def weight(r, l, g, x, cols):
    part = r.W[l, g, x, :, :, :, :, cols]
    return part.reshape(D, part.shape[-1])


def weight_rows(r, l, g, x, n, cols):
    per = r.W.shape[3] // 2
    part = r.W[l, g, x, pl.ds(n * per, per), :, :, :, cols]
    return part.reshape(HALF, part.shape[-1])


def put_grad(r, l, g, x, cols, value):
    lead = r.G.shape[3:7]
    r.G[l, g, x, :, :, :, :, cols] = value.astype(BF16).reshape(lead + value.shape[-1:])


def norm_into(r, l, src, normed, rstd_ref, gain, shift, out):
    def body(rows, carry):
        s = src[rows, :]
        centre = s - jnp.mean(s, -1, keepdims=True)
        rstd = lax.rsqrt(jnp.mean(centre * centre, -1, keepdims=True) + EPS)
        n = centre * rstd
        normed[l, rows, :] = n
        rstd_ref[l, rows, :] = rstd
        out[rows, :] = (n * gain[l] + shift[l]).astype(BF16)
        return carry

    row_loop(body, 0)


def norm_back(r, l, grad_y, normed, rstd_ref, gain, base, out, out_low):
    def body(rows, carry):
        gain_sum, shift_sum, out_sum = carry
        gy = grad_y[rows, :]
        n = normed[l, rows, :]
        e = gy * gain[l]
        back = rstd_ref[l, rows, :] * (
            e - jnp.mean(e, -1, keepdims=True) - n * jnp.mean(e * n, -1, keepdims=True)
        )
        res = base[rows, :] + back
        out[rows, :] = res
        out_low[rows, :] = res.astype(BF16)
        return (
            gain_sum + jnp.sum(gy * n, 0, keepdims=True),
            shift_sum + jnp.sum(gy, 0, keepdims=True),
            out_sum + jnp.sum(res, 0, keepdims=True),
        )

    zero = jnp.zeros((1, D), F32)
    return row_loop(body, (zero, zero, zero))


def to_windows(r, l):
    tok = lax.broadcasted_iota(jnp.int32, (WROWS, ROWS), 1)
    return jnp.where(tok == r.idx_col[l], 1.0, 0.0).astype(BF16)


def to_grid(r, l):
    tok = lax.broadcasted_iota(jnp.int32, (ROWS, WROWS), 0)
    return jnp.where(tok == r.idx_row[l], 1.0, 0.0).astype(BF16)


def cell_place(j):
    return (2 * WIN - 1) * (j // WIN) + j % WIN


def cell_pick(shape, cell_axis):
    cell = lax.broadcasted_iota(jnp.int32, shape, cell_axis)
    place = lax.broadcasted_iota(jnp.int32, shape, 1 - cell_axis)
    row = lax.shift_right_logical(cell * 37, 8)
    hit = (place == cell + 6 * row) & (cell < CELLS)
    return jnp.where(hit, 1.0, 0.0)


def dot_exact(a, b):
    return lax.dot_general(
        a, b, (((1,), (0,)), ((), ())), precision=lax.Precision.HIGHEST, preferred_element_type=F32
    )


LAST_PLACE = cell_place(CELLS - 1)


def expand_bias(r, l):
    pick = cell_pick((128, PADC), 1)
    live = lax.broadcasted_iota(jnp.int32, (PADC, PADC), 0) < CELLS
    r.ES[...] = jnp.zeros_like(r.ES)
    for x in range(2):
        table = r.SM[x, l, 8:16, :HALF]
        for j in range(CELLS):
            turn = (HALF - (LAST_PLACE - cell_place(j))) % HALF
            turned = pltpu.roll(table, turn, 1) if turn else table
            r.ES[j, 8 * x : 8 * x + 8, :] = turned[:, :128]
    for h in range(16):
        square = dot_exact(r.ES[:, h, :], pick)
        r.bias[l, h // 4, :, (h % 4) * PADC : (h % 4 + 1) * PADC] = jnp.where(live, square, MASKED)


def table_grads(r, l):
    pick = cell_pick((PADC, 128), 0)
    for h in range(16):
        part = r.DS[h // 4, :, (h % 4) * PADC : (h % 4 + 1) * PADC]
        r.ES[:, h, :] = dot_exact(part, pick)
    total = jnp.zeros((16, HALF), F32)
    zero = jnp.zeros((16, 128), F32)
    for j in range(CELLS):
        wide = jnp.concatenate([r.ES[j], zero], axis=1)
        turn = LAST_PLACE - cell_place(j)
        total = total + (pltpu.roll(wide, turn, 1) if turn else wide)
    r.AR[l, 16:32, :HALF] = total
    r.AR[l, 16:32, HALF:] = jnp.zeros((16, HALF), F32)


def attention_forward(r, l):
    def window(w, carry):
        rows = pl.ds(pl.multiple_of(w * PADC, PADC), PADC)
        pos = lax.rem(w, 4)
        same = r.reg_col[l, pos] == r.reg_row[l, pos]
        for g in range(4):
            lanes = slice(g * 128, (g + 1) * 128)
            q, k, v = r.Q[l, rows, lanes], r.K[l, rows, lanes], r.V[l, rows, lanes]
            s = dot_nt(k, spread_heads(q)) + r.bias[l, g]
            s = jnp.where(same, s, MASKED)
            e = jnp.exp(s - jnp.max(s, 0, keepdims=True))
            p = (e / jnp.sum(e, 0, keepdims=True)).astype(BF16)
            r.PR[l, w * 4 + g] = p
            r.AW[rows, lanes] = gather_heads(dot_tn(p, v)).astype(BF16)
        return carry

    lax.fori_loop(0, OWN * 4, window, 0)


def attention_backward(r, l, during):
    zero = jnp.zeros((1, 128), F32)

    def window(w, carry):
        during(w)
        rows = pl.ds(pl.multiple_of(w * PADC, PADC), PADC)
        sums = list(carry)
        for g in range(4):
            lanes = slice(g * 128, (g + 1) * 128)
            q, k, v = r.Q[l, rows, lanes], r.K[l, rows, lanes], r.V[l, rows, lanes]
            da = r.AW[rows, lanes]
            p = r.PR[l, w * 4 + g]
            da_spread = spread_heads(da)
            pf = p.astype(F32)
            pg = dot_nt(v, da_spread)
            ds = pf * (pg - jnp.sum(pf * pg, 0, keepdims=True))
            r.DS[g] += ds
            low = ds.astype(BF16)
            dv = dot(p, da_spread)
            dk = dot(low, spread_heads(q))
            dq = gather_heads(dot_tn(low, k)) * SCALE_Q
            r.Q[l, rows, lanes] = dq.astype(BF16)
            r.K[l, rows, lanes] = dk.astype(BF16)
            r.V[l, rows, lanes] = dv.astype(BF16)
            sums[g] = sums[g] + jnp.sum(dq, 0, keepdims=True)
            sums[4 + g] = sums[4 + g] + jnp.sum(dv, 0, keepdims=True)
        return tuple(sums)

    return lax.fori_loop(0, OWN * 4, window, (zero,) * 8)


def skip(*args):
    return None


IDLE = types.SimpleNamespace(need=skip, mlp=skip, mlp_done=skip, window=skip, attention_done=skip)


def forward(r, l, hooks):
    norm_into(r, l, r.S, r.N1, r.R1, r.ln1_gain, r.ln1_bias, r.YB)
    r.YW[l] = dot(to_windows(r, l), r.YB[...]).astype(BF16)
    hooks.need(l, 0)
    yw = r.YW[l]
    for x in range(2):
        cols = slice(x * HALF, (x + 1) * HALF)
        q = dot(yw, weight(r, l, 0, x, slice(0, HALF)))
        r.Q[l, :, cols] = ((q + r.SM[x, l, 1:2, :HALF]) * SCALE_Q).astype(BF16)
        r.K[l, :, cols] = dot(yw, weight(r, l, 0, x, slice(HALF, 2 * HALF))).astype(BF16)
        v = dot(yw, weight(r, l, 0, x, slice(2 * HALF, 3 * HALF)))
        r.V[l, :, cols] = (v + r.SM[x, l, 1:2, HALF : 2 * HALF]).astype(BF16)
    attention_forward(r, l)
    r.AT[l] = dot(to_grid(r, l), r.AW[...]).astype(BF16)
    for n in range(2):
        cols = slice(n * HALF, (n + 1) * HALF)
        acc = dot_nt(r.AT[l, :, :HALF], weight_rows(r, l, 0, 0, n, slice(3 * HALF, 4 * HALF)))
        acc += dot_nt(r.AT[l, :, HALF:], weight_rows(r, l, 0, 1, n, slice(3 * HALF, 4 * HALF)))
        r.S[:, cols] = r.S[:, cols] + acc + r.proj_bias[l, :, cols]
    norm_into(r, l, r.S, r.N2, r.R2, r.ln2_gain, r.ln2_bias, r.YB)
    r.Y2[l] = r.YB[...]
    hooks.need(l, 1)
    for x in range(2):

        def up(n, carry):
            at = pl.ds(pl.multiple_of(n * HALF, HALF), HALF)
            full = pl.ds(pl.multiple_of(x * 1024 + n * HALF, HALF), HALF)
            pre = dot(r.YB[...], weight(r, l, 1, x, at)) + r.SM[x, l, 0:1, at]
            phi = 0.5 * (1.0 + lax.erf(pre * INV_ROOT_TWO))
            r.AC[l, :, full] = (pre * phi).astype(BF16)
            dens = jnp.exp(-0.5 * pre * pre) * INV_ROOT_TWOPI
            r.SL[l, :, full] = (phi + pre * dens).astype(BF16)
            return carry

        lax.fori_loop(0, 4, up, 0)
    hooks.need(l, 2)
    for n in range(2):
        cols = slice(n * HALF, (n + 1) * HALF)
        acc = dot_nt(r.AC[l, :, :1024], weight_rows(r, l, 2, 0, n, slice(0, 1024)))
        acc += dot_nt(r.AC[l, :, 1024:], weight_rows(r, l, 2, 1, n, slice(0, 1024)))
        r.S[:, cols] = r.S[:, cols] + acc + r.fc2_bias[l, :, cols]


def backward_mlp(r, l, hooks):
    def low(rows, total):
        g = r.S[rows, :]
        r.YB[rows, :] = g.astype(BF16)
        return total + jnp.sum(g, 0, keepdims=True)

    r.AR[l, 9:10, :] = row_loop(low, jnp.zeros((1, D), F32))
    r.TA[...] = r.YB[...].T
    r.TB[:, :ROWS] = r.Y2[l].T
    for x in range(2):

        def down(n, carry):
            hooks.mlp(l, x * 4 + n)
            at = pl.ds(pl.multiple_of(n * HALF, HALF), HALF)
            full = pl.ds(pl.multiple_of(x * 1024 + n * HALF, HALF), HALF)
            pg = dot(r.YB[...], weight(r, l, 2, x, at)) * r.SL[l, :, full].astype(F32)
            r.F1[0:1, full] = jnp.sum(pg, 0, keepdims=True)
            pb = pg.astype(BF16)
            r.SL[l, :, full] = pb
            put_grad(r, l, 2, x, at, dot(r.TA[...], r.AC[l, :, full]))
            put_grad(r, l, 1, x, at, dot(r.TB[:, :ROWS], pb))
            return carry

        lax.fori_loop(0, 4, down, 0)
    hooks.mlp_done(l)
    for row in range(4):
        r.AR[l, row : row + 1, :] = r.F1[0:1, row * D : (row + 1) * D]
    for n in range(2):
        cols = slice(n * HALF, (n + 1) * HALF)
        acc = dot_nt(r.SL[l, :, :1024], weight_rows(r, l, 1, 0, n, slice(0, 1024)))
        acc += dot_nt(r.SL[l, :, 1024:], weight_rows(r, l, 1, 1, n, slice(0, 1024)))
        r.GY[:, cols] = acc
    gain, shift, out = norm_back(r, l, r.GY, r.N2, r.R2, r.ln2_gain, r.S, r.S, r.YB)
    r.AR[l, 6:7, :] = gain
    r.AR[l, 7:8, :] = shift
    r.AR[l, 8:9, :] = out


def backward_attention(r, l, hooks):
    r.TA[...] = r.YB[...].T
    for x in range(2):
        cols = slice(x * HALF, (x + 1) * HALF)
        put_grad(r, l, 0, x, slice(3 * HALF, 4 * HALF), dot(r.TA[...], r.AT[l, :, cols]))
        att = dot(r.YB[...], weight(r, l, 0, x, slice(3 * HALF, 4 * HALF)))
        r.GB[:, cols] = att.astype(BF16)
    r.AW[...] = dot(to_windows(r, l), r.GB[...]).astype(BF16)
    r.DS[...] = jnp.zeros_like(r.DS)
    sums = attention_backward(r, l, lambda w: hooks.window(l, w))
    for g in range(4):
        r.AR[l, 10:11, g * 128 : (g + 1) * 128] = sums[g]
        r.AR[l, 11:12, g * 128 : (g + 1) * 128] = sums[4 + g]
    r.AR[l, 12:16, :] = jnp.zeros((4, D), F32)
    r.TB[...] = r.YW[l].T
    for x in range(2):
        half = slice(x * HALF, (x + 1) * HALF)
        for part, ref in enumerate((r.Q, r.K, r.V)):
            cols = slice(part * HALF, (part + 1) * HALF)
            put_grad(r, l, 0, x, cols, dot(r.TB[...], ref[l, :, half]))
    hooks.attention_done(l)
    for n in range(2):
        cols = slice(n * HALF, (n + 1) * HALF)
        acc = jnp.zeros((WROWS, HALF), F32)
        for x in range(2):
            half = slice(x * HALF, (x + 1) * HALF)
            for part, ref in enumerate((r.Q, r.K, r.V)):
                take = slice(part * HALF, (part + 1) * HALF)
                acc += dot_nt(ref[l, :, half], weight_rows(r, l, 0, x, n, take))
        r.AW[:, cols] = acc.astype(BF16)
    r.GY[...] = dot(to_grid(r, l), r.AW[...])
    gain, shift, _ = norm_back(r, l, r.GY, r.N1, r.R1, r.ln1_gain, r.S, r.S, r.YB)
    r.AR[l, 4:5, :] = gain
    r.AR[l, 5:6, :] = shift
    table_grads(r, l)


ROW_INPUTS = ("ln1_gain", "ln1_bias", "proj_bias", "ln2_gain", "ln2_bias", "fc2_bias")
INPUTS = ("x", "cot", "valid", "idx_col", "idx_row", "reg_col", "reg_row") + ROW_INPUTS
SMALL = 32


def scratch_spec():
    return dict(
        S=pltpu.VMEM((ROWS, D), F32),
        GY=pltpu.VMEM((ROWS, D), F32),
        YB=pltpu.VMEM((ROWS, D), BF16),
        GB=pltpu.VMEM((ROWS, D), BF16),
        N1=pltpu.VMEM((LAYERS, ROWS, D), F32),
        N2=pltpu.VMEM((LAYERS, ROWS, D), F32),
        R1=pltpu.VMEM((LAYERS, ROWS, 1), F32),
        R2=pltpu.VMEM((LAYERS, ROWS, 1), F32),
        YW=pltpu.VMEM((LAYERS, WROWS, D), BF16),
        Q=pltpu.VMEM((LAYERS, WROWS, D), BF16),
        K=pltpu.VMEM((LAYERS, WROWS, D), BF16),
        V=pltpu.VMEM((LAYERS, WROWS, D), BF16),
        PR=pltpu.VMEM((LAYERS, OWN * 16, PADC, 4 * PADC), BF16),
        AW=pltpu.VMEM((WROWS, D), BF16),
        AT=pltpu.VMEM((LAYERS, ROWS, D), BF16),
        Y2=pltpu.VMEM((LAYERS, ROWS, D), BF16),
        AC=pltpu.VMEM((LAYERS, ROWS, FF), BF16),
        SL=pltpu.VMEM((LAYERS, ROWS, FF), BF16),
        TA=pltpu.VMEM((D, ROWS), BF16),
        TB=pltpu.VMEM((D, WROWS), BF16),
        ES=pltpu.VMEM((PADC, 16, 128), F32),
        DS=pltpu.VMEM((4, PADC, 4 * PADC), F32),
        bias=pltpu.VMEM((LAYERS, 4, PADC, 4 * PADC), F32),
        F1=pltpu.VMEM((1, FF), F32),
    )


def plain_kernel(names, *refs):
    r = types.SimpleNamespace(**dict(zip(names, refs)))
    r.S[...] = r.x[...].astype(F32)

    def ahead(l, c):
        expand_bias(r, l)
        forward(r, l, IDLE)
        return c

    lax.fori_loop(0, LAYERS, ahead, 0)
    r.result[...] = (r.S[...] * r.valid[...]).astype(BF16)
    r.S[...] = r.cot[...].astype(F32) * r.valid[...]

    def back(i, c):
        l = LAYERS - 1 - i
        backward_mlp(r, l, IDLE)
        backward_attention(r, l, IDLE)
        return c

    lax.fori_loop(0, LAYERS, back, 0)
    r.gimg[...] = r.YB[...]


def vmem_specs(n):
    return [pl.BlockSpec(memory_space=pltpu.VMEM)] * n


def plain_call(ins, small, w):
    outs = dict(
        G=jax.ShapeDtypeStruct(w.shape, BF16),
        AR=jax.ShapeDtypeStruct((LAYERS, SMALL, D), F32),
        result=jax.ShapeDtypeStruct((ROWS, D), BF16),
        gimg=jax.ShapeDtypeStruct((ROWS, D), BF16),
    )
    scratch = scratch_spec()
    names = INPUTS + ("SM", "W") + tuple(outs) + tuple(scratch)
    got = pl.pallas_call(
        functools.partial(plain_kernel, names),
        out_shape=list(outs.values()),
        in_specs=vmem_specs(len(INPUTS) + 2),
        out_specs=vmem_specs(len(outs)),
        scratch_shapes=list(scratch.values()),
        compiler_params=pltpu.CompilerParams(vmem_limit_bytes=67043328),
        name="step",
    )(*[ins[name] for name in INPUTS], small, w)
    return dict(zip(outs, got))


def kernel_inputs(images, cot, load, mp, rows):
    idx, reg = token_maps()
    keep = OWN * TOK_IMG

    def own(arr):
        slots = lax.dynamic_slice_in_dim(arr.swapaxes(0, 1), mp * OWN, OWN, 1)
        return jnp.pad(slots.reshape(keep, D), ((0, ROWS - keep), (0, 0)))

    at = jnp.arange(ROWS, dtype=jnp.int32)
    live = (mp * OWN + at % OWN < load) & (at < keep)
    ins = dict(
        x=own(images), cot=own(cot), valid=live.astype(F32)[:, None],
        idx_col=jnp.asarray(idx)[:, :, None], idx_row=jnp.asarray(idx)[:, None, :],
        reg_col=jnp.asarray(reg)[:, :, :, None],
        reg_row=jnp.asarray(np.tile(reg, (1, 1, 4)))[:, :, None, :],
    )
    ins.update({name: a.reshape(LAYERS, 1, -1) for name, a in rows.items()})
    return ins


def pack_small(fc1_bias, qv_bias, rel_table):
    wide = lambda a: jnp.pad(a, ((0, 0), (0, 0), (0, 1024 - a.shape[2])))
    return jnp.concatenate(
        [
            fc1_bias.reshape(LAYERS, 1, 1024),
            wide(qv_bias.reshape(LAYERS, 1, 2 * HALF)),
            jnp.zeros((LAYERS, 6, 1024), F32),
            wide(rel_table),
        ],
        1,
    )


def pack_weights(w_qkv, w_proj, w_fc1, w_fc2):
    rows = w_qkv.shape[1]
    first = jnp.concatenate([w_qkv.reshape(LAYERS, rows, -1), w_proj.swapaxes(1, 2)], 2)
    return jnp.stack([first, w_fc1, w_fc2.swapaxes(1, 2)], 1)


MESH = pl.DeviceIdType.MESH
UNITS = 3 * LAYERS
Z_SIDE = 4


class Place:
    def __init__(self):
        self.dp = lax.axis_index("dp")
        self.x = lax.axis_index("mp")
        self.c = lax.rem(self.dp, 2)
        self.y = lax.rem(self.dp // 2, 2)
        self.z = self.dp // 4
        self.sib = {"dp": self.dp + 1 - 2 * self.c, "mp": self.x}
        self.ynbr = {"dp": self.dp + 2 - 4 * self.y, "mp": self.x}
        self.xnbr = {"dp": self.dp, "mp": 1 - self.x}

    def zpos(self, k):
        return lax.rem(self.z + k, Z_SIDE)

    def zpeer(self, k):
        return {"dp": self.zpos(k) * 4 + lax.rem(self.dp, 4), "mp": self.x}

    def peers(self):
        return [self.sib, self.ynbr, self.xnbr] + [self.zpeer(k) for k in range(1, Z_SIDE)]


def greet(place):
    barrier = pltpu.get_barrier_semaphore()
    peers = place.peers()
    for peer in peers:
        pl.semaphore_signal(barrier, inc=1, device_id=peer, device_id_type=MESH)
    pl.semaphore_wait(barrier, len(peers))


def remote(src, dst, sems, u, k, peer):
    return pltpu.make_async_remote_copy(
        src_ref=src, dst_ref=dst, send_sem=sems.at[0, u, k], recv_sem=sems.at[1, u, k],
        device_id=peer, device_id_type=MESH,
    )


def landed(dst, sems, u, k, peer):
    remote(dst, dst, sems, u, k, peer).wait_recv()


TOP, LOW = pl.ds(0, 16), pl.ds(16, 16)


class Gather:
    def __init__(self, place, shard, w, sems, local):
        self.p, self.shard, self.w, self.sems, self.local = place, shard, w, sems, local

    def slab(self, u, x, y, c, part=None):
        ref = self.w.at[u // 3, lax.rem(u, 3), x, :, y, c]
        return ref if part is None else ref.at[:, part]

    def block(self, u, z):
        p = self.p
        return self.w.at[u // 3, lax.rem(u, 3), p.x, z, p.y, p.c]

    def own(self, u):
        return self.shard.at[u // 3, lax.rem(u, 3)]

    def z_copy(self, u, k):
        return remote(self.own(u), self.block(u, self.p.z), self.sems, u, k - 1, self.p.zpeer(k))

    def local_copy(self, u):
        return pltpu.make_async_copy(self.own(u), self.block(u, self.p.z), self.local.at[u])

    def full_copies(self, u):
        p = self.p
        mine = self.slab(u, p.x, p.y, p.c)
        return [
            remote(mine, mine, self.sems, u, 3, p.xnbr),
            remote(mine, mine, self.sems, u, 4, p.ynbr),
            remote(mine, mine, self.sems, u, 5, p.sib),
        ]

    def half_copies(self, u):
        p = self.p
        from_y, from_x = (p.x, 1 - p.y, p.c), (1 - p.x, p.y, p.c)
        top, low = self.slab(u, *from_y, TOP), self.slab(u, *from_x, LOW)
        fy, fx = self.slab(u, *from_y), self.slab(u, *from_x)
        return [
            remote(top, top, self.sems, u, 6, p.xnbr),
            remote(low, low, self.sems, u, 7, p.ynbr),
            remote(fx, fx, self.sems, u, 8, p.sib),
            remote(fy, fy, self.sems, u, 9, p.sib),
        ]

    def last_copies(self, u):
        p = self.p
        far = self.slab(u, 1 - p.x, 1 - p.y, p.c)
        return [remote(far, far, self.sems, u, 10, p.sib)]

    def start_own(self, u):
        self.local_copy(u).start()
        for k in range(1, Z_SIDE):
            self.z_copy(u, k).start()

    def pass_own(self, u):
        p = self.p
        self.local_copy(u).wait()
        for k in range(1, Z_SIDE):
            landed(self.block(u, p.zpos(Z_SIDE - k)), self.sems, u, k - 1, p.zpeer(Z_SIDE - k))
        for copy in self.full_copies(u):
            copy.start()

    def pass_near(self, u):
        p = self.p
        landed(self.slab(u, 1 - p.x, p.y, p.c), self.sems, u, 3, p.xnbr)
        landed(self.slab(u, p.x, 1 - p.y, p.c), self.sems, u, 4, p.ynbr)
        for copy in self.half_copies(u):
            copy.start()

    def pass_far(self, u):
        p = self.p
        landed(self.slab(u, 1 - p.x, 1 - p.y, p.c, TOP), self.sems, u, 6, p.xnbr)
        landed(self.slab(u, 1 - p.x, 1 - p.y, p.c, LOW), self.sems, u, 7, p.ynbr)
        for copy in self.last_copies(u):
            copy.start()

    def ready(self, u):
        p = self.p
        for k, (x, y) in ((5, (p.x, p.y)), (8, (1 - p.x, p.y)), (9, (p.x, 1 - p.y)), (10, (1 - p.x, 1 - p.y))):
            landed(self.slab(u, x, y, 1 - p.c), self.sems, u, k, p.sib)

    def tick(self, t):
        @pl.when(t < UNITS)
        def _():
            self.pass_own(t)

        @pl.when(t + 2 < UNITS)
        def _():
            self.start_own(t + 2)

        @pl.when((t >= 1) & (t - 1 < UNITS))
        def _():
            self.pass_near(t - 1)

        @pl.when((t >= 2) & (t - 2 < UNITS))
        def _():
            self.pass_far(t - 2)

    def drain(self, u):
        for k in range(1, Z_SIDE):
            self.z_copy(u, k).wait_send()
        for copy in self.full_copies(u) + self.half_copies(u) + self.last_copies(u):
            copy.wait_send()


class Scatter:
    def __init__(self, place, r):
        self.p, self.r, self.sems = place, r, r.sums

    def buf(self, ref, u):
        return ref.at[lax.rem(u, 3)]

    def grads(self, u):
        return self.r.G.at[u // 3, lax.rem(u, 3)]

    def sib_copy(self, u):
        p = self.p
        src = self.grads(u).at[:, :, :, 1 - p.c]
        return remote(src, self.buf(self.r.P, u), self.sems, u, 0, p.sib)

    def part(self, u, x, y, rows=None):
        ref = self.buf(self.r.P, u).at[x, :, y]
        return ref if rows is None else ref.at[:, rows]

    def far_copies(self, u):
        p, into = self.p, self.buf(self.r.RA, u)
        return [
            remote(self.part(u, 1 - p.x, 1 - p.y, TOP), into.at[0], self.sems, u, 1, p.xnbr),
            remote(self.part(u, 1 - p.x, 1 - p.y, LOW), into.at[1], self.sems, u, 2, p.ynbr),
        ]

    def near_copies(self, u):
        p, into = self.p, self.buf(self.r.RB, u)
        return [
            remote(self.part(u, 1 - p.x, p.y), into.at[0], self.sems, u, 3, p.xnbr),
            remote(self.part(u, p.x, 1 - p.y), into.at[1], self.sems, u, 4, p.ynbr),
        ]

    def z_copy(self, u, k):
        p = self.p
        src = self.buf(self.r.P, u).at[p.x, p.zpos(k), p.y]
        return remote(src, self.buf(self.r.RC, u).at[k - 1], self.sems, u, 4 + k, p.zpeer(k))

    def add(self, dst, *srcs):
        def step(z, c):
            total = dst[z].astype(F32)
            for src in srcs:
                total = total + src[z].astype(F32)
            dst[z] = total.astype(BF16)
            return c

        lax.fori_loop(0, Z_SIDE, step, 0)

    def sib(self, u):
        self.sib_copy(u).start()

    def far(self, u):
        p = self.p
        landed(self.buf(self.r.P, u), self.sems, u, 0, p.sib)
        grads = self.grads(u)
        self.add(self.part(u, 1 - p.x, 1 - p.y), grads.at[1 - p.x, :, 1 - p.y, p.c])
        for copy in self.far_copies(u):
            copy.start()
        for x, y in ((1 - p.x, p.y), (p.x, 1 - p.y), (p.x, p.y)):
            self.add(self.part(u, x, y), grads.at[x, :, y, p.c])

    def near(self, u):
        p, got = self.p, self.buf(self.r.RA, u)
        landed(got.at[0], self.sems, u, 1, p.xnbr)
        landed(got.at[1], self.sems, u, 2, p.ynbr)
        self.add(self.part(u, p.x, 1 - p.y, TOP), got.at[0])
        self.add(self.part(u, 1 - p.x, p.y, LOW), got.at[1])
        for copy in self.near_copies(u):
            copy.start()

    def z(self, u):
        p, got = self.p, self.buf(self.r.RB, u)
        landed(got.at[0], self.sems, u, 3, p.xnbr)
        landed(got.at[1], self.sems, u, 4, p.ynbr)
        self.add(self.part(u, p.x, p.y), got.at[0], got.at[1])
        for k in range(1, Z_SIDE):
            self.z_copy(u, k).start()

    def finish(self, u):
        p, r = self.p, self.r
        total = r.P[lax.rem(u, 3), p.x, p.z, p.y].astype(F32)
        for k in range(1, Z_SIDE):
            landed(self.buf(r.RC, u).at[k - 1], self.sems, u, 4 + k, p.zpeer(Z_SIDE - k))
            total = total + r.RC[lax.rem(u, 3), k - 1].astype(F32)
        r.grad[u // 3, lax.rem(u, 3)] = total
        for copy in [self.sib_copy(u)] + self.far_copies(u) + self.near_copies(u):
            copy.wait_send()
        for k in range(1, Z_SIDE):
            self.z_copy(u, k).wait_send()

    def release(self, g):
        for peer in self.p.peers():
            pl.semaphore_signal(self.r.free.at[g], inc=1, device_id=peer, device_id_type=MESH)

    def claim(self, g):
        pl.semaphore_wait(self.r.free.at[g], len(self.p.peers()))


class Total:
    def __init__(self, place, r):
        self.p, self.r, self.sems = place, r, r.totals

    def copy(self, l, k):
        p, r = self.p, self.r
        if k < 3:
            src = r.AR.at[l] if k == 0 else r.AS.at[l, k - 1]
            return remote(src, r.AB.at[l, k], self.sems, l, k, (p.sib, p.xnbr, p.ynbr)[k])
        hop = k - 2
        return remote(r.AS.at[l, 2], r.AZ.at[l, p.z], self.sems, l, k, p.zpeer(hop))

    def step(self, l, k):
        p, r = self.p, self.r
        if k:
            landed(r.AB.at[l, k - 1], self.sems, l, k - 1, (p.sib, p.xnbr, p.ynbr)[k - 1])
            mine = r.AR[l] if k == 1 else r.AS[l, k - 2]
            total = mine + r.AB[l, k - 1]
            r.AS[l, k - 1] = total
        if k < 3:
            self.copy(l, k).start()
        else:
            r.AZ[l, p.z] = total
            for hop in range(1, Z_SIDE):
                self.copy(l, 2 + hop).start()

    def finish(self, l):
        p, r = self.p, self.r
        for hop in range(1, Z_SIDE):
            from_z = p.zpos(Z_SIDE - hop)
            landed(r.AZ.at[l, from_z], self.sems, l, 2 + hop, p.zpeer(Z_SIDE - hop))
        total = r.AZ[l, 0]
        for z in range(1, Z_SIDE):
            total = total + r.AZ[l, z]
        r.small_sum[l] = total
        for k in range(2 + Z_SIDE):
            self.copy(l, k).wait_send()


def comm_scratch():
    return dict(
        W=pltpu.VMEM((LAYERS, 3, 2, Z_SIDE, 2, 2, 32, 1024), BF16),
        G=pltpu.VMEM((LAYERS, 3, 2, Z_SIDE, 2, 2, 32, 1024), BF16),
        P=pltpu.VMEM((3, 2, Z_SIDE, 2, 32, 1024), BF16),
        RA=pltpu.VMEM((3, 2, Z_SIDE, 16, 1024), BF16),
        RB=pltpu.VMEM((3, 2, Z_SIDE, 32, 1024), BF16),
        RC=pltpu.VMEM((3, Z_SIDE - 1, 32, 1024), BF16),
        SM=pltpu.VMEM((2, LAYERS, 16, 1024), F32),
        AR=pltpu.VMEM((LAYERS, SMALL, D), F32),
        AB=pltpu.VMEM((LAYERS, 3, SMALL, D), F32),
        AS=pltpu.VMEM((LAYERS, 3, SMALL, D), F32),
        AZ=pltpu.VMEM((LAYERS, Z_SIDE, SMALL, D), F32),
        gathers=pltpu.SemaphoreType.DMA((2, UNITS, 11)),
        local=pltpu.SemaphoreType.DMA((UNITS + 1,)),
        sums=pltpu.SemaphoreType.DMA((2, UNITS, 8)),
        totals=pltpu.SemaphoreType.DMA((2, LAYERS, 6)),
        swaps=pltpu.SemaphoreType.DMA((2, 1, 3)),
        free=pltpu.SemaphoreType.REGULAR((3,)),
    )


def fused_kernel(names, *refs):
    r = types.SimpleNamespace(**dict(zip(names, refs)))
    place = Place()
    x = place.x
    gather = Gather(place, r.shard, r.W, r.gathers, r.local)
    scatter = Scatter(place, r)
    total = Total(place, r)

    def swap(src, ref, k):
        return remote(src, ref.at[x], r.swaps, 0, k, place.xnbr)

    greet(place)
    gather.start_own(0)
    swap(r.small, r.SM, 0).start()
    own_small = pltpu.make_async_copy(r.small, r.SM.at[x], r.local.at[UNITS])
    own_small.start()
    gather.start_own(1)
    r.S[...] = r.x[...].astype(F32)
    own_small.wait()
    landed(r.SM.at[1 - x], r.swaps, 0, 0, place.xnbr)
    swap(r.small, r.SM, 0).wait_send()

    def opening(l, c):
        gather.tick(l)
        expand_bias(r, l)
        return c

    lax.fori_loop(0, LAYERS, opening, 0)

    def need(l, g):
        gather.tick(3 * l + g + 2)
        gather.ready(3 * l + g)

    ahead = types.SimpleNamespace(need=need)

    def forward_step(l, c):
        forward(r, l, ahead)
        return c

    lax.fori_loop(0, LAYERS, forward_step, 0)
    r.result[x] = (r.S[...] * r.valid[...]).astype(BF16)
    r.S[...] = r.cot[...].astype(F32) * r.valid[...]

    def drain(u, c):
        gather.drain(u)
        return c

    lax.fori_loop(0, UNITS, drain, 0)
    swap(r.result.at[x], r.result, 1).start()

    def at(cond, *acts):
        @pl.when(cond)
        def _():
            for act in acts:
                act()

    def mlp(l, k):
        low = l == 0
        at(low & (k == 1), lambda: scatter.finish(5), lambda: scatter.release(2))
        at(low & (k == 2), lambda: scatter.near(3))
        at(low & (k == 3), lambda: scatter.finish(4), lambda: scatter.release(1))
        at(low & (k == 4), lambda: total.step(1, 1))
        at(low & (k == 6), lambda: total.step(1, 2))

    def mlp_done(l):
        at(l == 0, lambda: scatter.z(3), lambda: scatter.claim(2))
        scatter.sib(3 * l + 2)
        at(l == 0, lambda: scatter.claim(1))
        scatter.sib(3 * l + 1)

    def window(l, w):
        low = l == 0
        at(w == 0, lambda: scatter.far(3 * l + 2))
        at(low & (w == 1), lambda: total.step(1, 3))
        at(w == 2, lambda: scatter.far(3 * l + 1))
        at(low & (w == 3), lambda: scatter.finish(3), lambda: scatter.release(0))
        at(w == 4, lambda: scatter.near(3 * l + 2))
        at(low & (w == 5), lambda: total.finish(1))
        at(w == 7, lambda: scatter.near(3 * l + 1))

    def attention_done(l):
        at(l == 0, lambda: scatter.claim(0))
        scatter.sib(3 * l)
        scatter.z(3 * l + 2)

    hooks = types.SimpleNamespace(
        mlp=mlp, mlp_done=mlp_done, window=window, attention_done=attention_done
    )

    def backward_step(i, c):
        l = LAYERS - 1 - i
        backward_mlp(r, l, hooks)
        backward_attention(r, l, hooks)
        scatter.z(3 * l + 1)
        scatter.far(3 * l)
        total.step(l, 0)
        return c

    lax.fori_loop(0, LAYERS, backward_step, 0)
    r.gimg[x] = r.YB[...]
    scatter.finish(2)
    scatter.near(0)
    swap(r.gimg.at[x], r.gimg, 2).start()
    total.step(0, 1)
    scatter.finish(1)
    total.step(0, 2)
    scatter.z(0)
    total.step(0, 3)
    scatter.finish(0)
    total.finish(0)
    for k, ref in ((1, r.result), (2, r.gimg)):
        landed(ref.at[1 - x], r.swaps, 0, k, place.xnbr)
        swap(ref.at[x], ref, k).wait_send()


def fused_call(ins, small, shard):
    outs = dict(
        grad=jax.ShapeDtypeStruct((LAYERS, 3, 32, 1024), F32),
        small_sum=jax.ShapeDtypeStruct((LAYERS, SMALL, D), F32),
        result=jax.ShapeDtypeStruct((2, ROWS, D), BF16),
        gimg=jax.ShapeDtypeStruct((2, ROWS, D), BF16),
    )
    scratch = scratch_spec() | comm_scratch()
    names = INPUTS + ("small", "shard") + tuple(outs) + tuple(scratch)
    got = pl.pallas_call(
        functools.partial(fused_kernel, names),
        out_shape=list(outs.values()),
        in_specs=vmem_specs(len(INPUTS) + 2),
        out_specs=vmem_specs(len(outs)),
        scratch_shapes=list(scratch.values()),
        compiler_params=pltpu.CompilerParams(
            collective_id=0, has_side_effects=True, vmem_limit_bytes=67043328
        ),
        name="step",
    )(*[ins[name] for name in INPUTS], small, shard)
    return dict(zip(outs, got))


def gather_plain(shard):
    full = lax.all_gather(shard, "dp", axis=2, tiled=True)
    return lax.all_gather(full, "mp", axis=2, tiled=False)


def scatter_plain(grad):
    half = lax.psum_scatter(grad, "mp", scatter_dimension=2, tiled=False)
    return lax.psum_scatter(half, "dp", scatter_dimension=2, tiled=True).astype(F32)


def collective_call(ins, small, shard):
    full = gather_plain(shard).reshape(LAYERS, 3, 2, 4, 1, 1, D // 4, 1024)
    outs = plain_call(ins, lax.all_gather(small, "mp"), full)
    return dict(
        grad=scatter_plain(outs["G"].reshape(LAYERS, 3, 2, D, 1024)),
        small_sum=lax.psum(outs["AR"], ("dp", "mp")),
        result=lax.all_gather(outs["result"], "mp"),
        gimg=lax.all_gather(outs["gimg"], "mp"),
    )


def per_device(
    images, loads, cotangent, ln1_gain, ln1_bias, w_qkv, qv_bias, rel_table, w_proj, proj_bias,
    ln2_gain, ln2_bias, w_fc1, fc1_bias, w_fc2, fc2_bias,
):
    mp = lax.axis_index("mp")
    rows = dict(
        ln1_gain=ln1_gain, ln1_bias=ln1_bias, proj_bias=proj_bias, ln2_gain=ln2_gain,
        ln2_bias=ln2_bias, fc2_bias=fc2_bias,
    )
    ins = kernel_inputs(images, cotangent, loads[0], mp, rows)
    small = pack_small(fc1_bias, qv_bias, rel_table)
    shard = pack_weights(w_qkv, w_proj, w_fc1, w_fc2)
    direct = lax.axis_size("dp") == 4 * Z_SIDE and lax.axis_size("mp") == 2
    outs = (fused_call if direct else collective_call)(ins, small, shard)
    grad, sums = outs["grad"], outs["small_sum"]

    def whole(both):
        kept = both[:, : OWN * TOK_IMG].reshape(2, TOK_IMG, OWN, D)
        return kept.transpose(0, 2, 1, 3).reshape(2 * OWN, TOK_IMG, D)

    entries = rel_table.shape[2]
    return (
        whole(outs["result"]),
        whole(outs["gimg"]),
        sums[:, 4],
        sums[:, 5],
        grad[:, 0, :, : 3 * HALF].reshape(w_qkv.shape),
        lax.dynamic_slice_in_dim(sums[:, 10:12], mp * HALF, HALF, 2),
        lax.dynamic_slice_in_dim(sums[:, 16:32], mp * 8, 8, 1)[:, :, :entries],
        grad[:, 0, :, 3 * HALF :].swapaxes(1, 2),
        sums[:, 8],
        sums[:, 6],
        sums[:, 7],
        grad[:, 1],
        lax.dynamic_slice_in_dim(sums[:, :4].reshape(LAYERS, FF), mp * 1024, 1024, 1),
        grad[:, 2].swapaxes(1, 2),
        sums[:, 9],
    )


def solution(mesh):
    wq, cols = P(None, "dp", None, "mp"), P(None, "mp")
    rows_dp, cols_dp = P(None, "dp", "mp"), P(None, "mp", "dp")
    img = P("dp", None, None)
    qv, tab = P(None, None, "mp"), P(None, "mp", None)
    return jax.shard_map(
        per_device,
        mesh=mesh,
        in_specs=(
            img, P("dp"), img, P(), P(), wq, qv, tab, cols_dp, P(), P(), P(), rows_dp, cols, cols_dp, P(),
        ),
        out_specs=(img, img, P(), P(), wq, qv, tab, cols_dp, P(), P(), P(), rows_dp, cols, cols_dp, P()),
        check_vma=False,
    )
```

time: 364 us -> 213 us (0.59)
  blocking collectives: 53.2 us -> 0 us
  Pallas kernels: 233 us -> 180 us
  waiting for transfers between devices: 22.6 us -> 0 us
  between operations: 16.5 us -> 1.45 us
  matrix products: 5.34 us -> 0 us
    pallas_call x3 -> x1, Pallas kernels: 233 us -> 180 us  [fused_call(): pl.pallas_call(functools.partial(fused_kernel, names), out_shape=list(out...]
    psum x1 -> x0, blocking collectives: 39.8 us -> none  [per_device(): sg, tab = lax.psum((outs['SG'], table_grads(outs['DS'])), ('dp', 'mp'))]
    psum x1 -> x0, waiting for transfers between devices: 22.6 us -> none  [per_device(): sg, tab = lax.psum((outs['SG'], table_grads(outs['DS'])), ('dp', 'mp'))]
    all_gather x3 -> x0, blocking collectives: 13.4 us -> none  [the longest x1 4.54 us: per_device(): table_all = lax.all_gather(rel_table, 'mp', axis=1, tiled=True)]
    unnamed x49 -> x39, local copies, waits for them, and re-layouts: 14.1 us -> 7.99 us
    dot_general x2 -> x0, matrix products: 5.34 us -> none  [the longest x1 3.79 us: small_inputs(): lax.dot_general(onehot, rel_table.reshape(LAYERS * heads, entries), (((1,...]
  transfers between devices with their start and end apart: 2 -> 0, of which waited for: 1 -> 0; matrix products, arithmetic and copies ran while one was open for 4% -> 0% of each run, Pallas kernels for 24% -> 0%
where the time goes in v3:
time: 213 us
  Pallas kernels  180 us (85%)
  local copies, waits for them, and re-layouts  28.9 us (14%)
  other arithmetic  2.28 us (1%)
    pallas_call x1, Pallas kernels, fused_call(): pl.pallas_call(functools.partial(fused_kernel, names), out_shape=list(out...  180 us
    unnamed x39, local copies, waits for them, and re-layouts  7.99 us

profile of v3, /device:TPU:0, one launch (start us, length us, event | category | flops | bytes accessed | tf_op | source)
XLA Modules:
  0.0 212.6 jit_solution(3040713700845649428)
XLA Ops:
  0.6 2.2 %dynamic-slice_bitcast_fusion = (bf16[196,2,512]{2,1,0:T(2,128)(2,1)S(1)}, bf16[196,2,512]{2,1,0:T(2,128)(2,1)S(1)}) fusion(bf16[4,196,512]{2,0,1:T(4,128)(2,1)} %param.21, s32[]{:T(128)S(6)} %select_n.27, bf16[4,196,512]{2,0,1:T(4,128)(2,1)} %param.19), kind=kLoop, calls=%fused_computation | loop fusion | bytes 1605636 | tf_op jit(solution)/shard_map/dynamic_slice | solution.py:466
  2.9 0.2 reshape.118
  3.0 0.8 pad.15.refs_0_
  3.8 0.2 reshape.119
  4.0 0.8 pad.16.refs_1_
  5.4 0.7 fusion.5.refs_2_
  6.1 0.1 copy-done.4
  6.3 0.7 copy-done.5
  7.1 0.9 copy-done.2
  8.0 0.8 pad_maximum_fusion.refs_14_
  9.0 0.6 copy-done.6
  9.6 0.7 select_maximum_fusion.refs_13_
  10.3 0.6 reshape.120.refs_7_
  10.9 0.1 copy-done.10
  11.0 0.6 reshape.121.refs_8_
  11.6 0.1 copy-done.11
  11.7 0.6 reshape.122.refs_9_
  12.3 0.1 copy-done.12
  12.4 0.6 reshape.123.refs_10_
  13.0 0.1 copy-done.13
  13.1 0.6 reshape.124.refs_11_
  13.7 0.1 copy-done.14
  13.7 0.6 reshape.125.refs_12_
  14.3 180.0 %step.1 = (f32[2,3,32,1024]{3,2,1,0:T(8,128)}, f32[2,32,512]{2,1,0:T(8,128)}, bf16[2,400,512]{2,1,0:T(8,128)(2,1)}, bf16[2,400,512]{2,1,0:T(8,128)(2,1)}) custom-call(bf16[400,512]{1,0:T(8,128)(2,1)} %pad.15.refs_0_, bf16[400,512]{1,0:T(8,128)(2,1)} %pad.16.refs_1_, f32[400,1]{1,0:T(8,128)} %fusion.5.refs_2_, s32[2,512,1]{2,1,0:T(8,128)} %constant.62.refs_3_, ...), custom_call_target="tpu_custom_call" | custom-call | tf_op jit(solution)/shard_map/step/pallas_call | solution.py:934
  194.3 0.9 slice.54
  195.2 0.6 constant_dynamic-slice_fusion.1
  195.8 0.8 slice_bitcast_fusion.3
  196.5 0.6 constant_dynamic-slice_fusion
  197.2 0.8 slice.53
  197.9 0.6 constant_dynamic-slice_fusion.2
  198.5 1.0 fusion.9
  199.5 0.6 copy.64
  200.1 0.6 copy.65
  200.7 0.6 copy.66
  201.3 0.6 copy.67
  201.9 0.6 copy.68
  202.5 0.6 copy.69
  203.1 1.9 slice_bitcast_fusion
  205.0 1.0 slice.52
  206.0 0.1 reshape_squeeze.3
  206.1 0.7 copy.46
  206.8 1.5 slice_bitcast_fusion.2
  208.4 0.3 reshape.129
  208.7 0.6 copy.44
  209.2 1.2 reshape.130
  210.5 0.3 reshape.131
  210.8 0.6 copy.45
  211.4 1.2 reshape.132
  (30 shorter events, 0.3 us)
Async XLA Ops:
  5.4 0.9 copy-start.4
  6.3 0.8 copy-start.5
  7.1 0.9 copy-start.2
  7.1 1.0 copy-start.3
  8.0 0.8 copy-start.7
  8.0 0.8 copy-start.8
  8.8 0.7 copy-start.6
  9.6 0.7 copy-start.9
  10.3 0.7 copy-start.10
  11.0 0.7 copy-start.11
  11.7 0.7 copy-start.12
  12.4 0.7 copy-start.13
  13.1 0.7 copy-start.14
  205.0 3.3 %copy-start.1 = (bf16[2,400,512]{2,1,0:T(8,128)(2,1)S(1)}, bf16[2,400,512]{2,1,0:T(8,128)(2,1)}, u32[]{:S(2)}) copy-start(bf16[2,400,512]{2,1,0:T(8,128)(2,1)} %get-tuple-element.19) | copy-start | bytes 2457604
  209.2 1.2 copy-start
